TPU v7x, 32 devices: a whole 2x2x4 slice. The times are simulated.
32 devices in a mesh: outer: 4 (over x, core), chip: 8 (over z, y).
Axes of the slice: x: 2, y: 2, z: 4, core: 2. Of those that a mesh axis runs over, the one named last changes fastest.
Arguments:
- inputs: bfloat16 [4096, 2048], P(('outer', 'chip')), may hold values from -6 to 6
- out_grads: bfloat16 [4096, 2048], P(('outer', 'chip')), may hold values from -6 to 6
- weight: bfloat16 [2048, 2048], P('chip'), may hold values from -0.125 to 0.125
- start_basis: float32 [64, 2048], P('chip'), may hold values from -6 to 6
- error_buffer: float32 [4, 2048, 2048], P('outer', 'chip'), may hold values from -2 to 2
Outputs:
- outputs: bfloat16 [4096, 2048], P(('outer', 'chip'))
- new_error: float32 [4, 2048, 2048], P('outer', 'chip')
All inputs are finite; a program needn't handle non-finite values.
Results may differ from a plain program's by a relative error of at most 0.0085.
Values may be sent and summed in bfloat16 or wider, within the bound.
A program may use at most 128 MiB of HBM per device.

v0:
```python
import functools

import jax
import jax.numpy as jnp
from jax import lax
from jax.experimental import pallas as pl
from jax.experimental.pallas import tpu as pltpu
from jax.sharding import PartitionSpec as P

TOK_DEV = 128
LEARNING_RATE = 0.2
CHUNKS = 4
F32 = jnp.float32
BF16 = jnp.bfloat16


def dot(a, b, ca, cb):
    return lax.dot_general(
        a, b, (((ca,), (cb,)), ((), ())), preferred_element_type=F32
    )


def halves(v):
    high = v.astype(BF16).astype(F32)
    return high, v - high


def stack(*parts):
    return jnp.concatenate(parts, axis=0).astype(BF16)


def thin_dot(thin, wide, cb):
    n = thin.shape[0]
    thin_high, thin_low = halves(thin)
    wide_high, wide_low = halves(wide)
    both = dot(stack(thin_high, thin_low), wide_high.astype(BF16), 1, cb)
    return both[:n] + both[n:] + dot(thin_high.astype(BF16), wide_low.astype(BF16), 1, cb)


def orthonormal(v):
    count = v.shape[0]
    row = lax.broadcasted_iota(jnp.int32, (count, 1), 0)
    for k in range(count):
        pivot = v[k : k + 1, :]
        d = jnp.sum(v * pivot, axis=1, keepdims=True)
        norm = d[k : k + 1, :] + 1.0
        scale = jnp.where(row > k, d / norm, 0.0)
        unit = pivot / jnp.sqrt(norm)
        v = jnp.where(row == k, unit, v - scale * pivot)
    return v


def kernel(
    A, B, PODS,
    x_ref, g_ref, w_ref, basis_ref, err_ref,
    out_ref, ne_ref,
    xg, xt, gg, wq, ysend, yrecv, up_s, up_r, dn_s, dn_r,
    left_s, left_r, right_s, right_r, fl, fr, own,
    xs_sem, xr_sem, ws_sem, wr_sem, gs_sem, gr_sem, ys_sem, yr_sem, rs_sem, rr_sem,
    ls_sem, lr_sem, hs_sem, hr_sem, fs_sem, fq_sem,
):
    o = lax.axis_index("outer")
    c = lax.axis_index("chip")
    a, b = c // B, c % B
    NC = A * B
    T, N = g_ref.shape
    S = w_ref.shape[0]
    Q = B * S
    R = basis_ref.shape[0]
    K = CHUNKS
    CN = N // K
    cols = [pl.ds(k * CN, CN) for k in range(K)]

    def remote(src, dst, ss, rs, axis, index):
        return pltpu.make_async_remote_copy(
            src_ref=src, dst_ref=dst, send_sem=ss, recv_sem=rs,
            device_id={axis: index}, device_id_type=pl.DeviceIdType.MESH,
        )

    barrier = pltpu.get_barrier_semaphore()
    for d in range(1, NC):
        pl.semaphore_signal(
            barrier, inc=1, device_id={"chip": (c + d) % NC}, device_id_type=pl.DeviceIdType.MESH
        )
    for d in range(1, PODS):
        pl.semaphore_signal(
            barrier, inc=1, device_id={"outer": (o + d) % PODS}, device_id_type=pl.DeviceIdType.MESH
        )
    pl.semaphore_wait(barrier, NC - 1 + PODS - 1)

    def rows_of(s):
        return pl.ds(pl.multiple_of(s * T, T), T)

    def shard_of(s):
        return pl.ds(pl.multiple_of(s * S, S), S)

    x_copies = []
    for d in range(1, A):
        t = (a + d) % A
        x_copies.append(remote(
            x_ref.at[:, pl.ds(pl.multiple_of(t * Q, Q), Q)], xg.at[rows_of(a)],
            xs_sem.at[d], xr_sem.at[d], "chip", t * B + b,
        ))
    for cp in x_copies:
        cp.start()

    def g_copy(direction, h, k):
        step = 1 if direction == 0 else -1
        source = a - step * (h - 1)
        src = g_ref.at[:, cols[k]] if h == 1 else gg.at[rows_of(source), cols[k]]
        return remote(
            src, gg.at[rows_of(source), cols[k]],
            gs_sem.at[direction, h, k], gr_sem.at[direction, h, k], "chip", c + step * B,
        )

    def g_sends(direction, h):
        return (
            jnp.logical_and(a - (h - 1) >= 0, a + 1 < A)
            if direction == 0
            else jnp.logical_and(a + (h - 1) < A, a >= 1)
        )

    def g_gets(direction, h):
        return a - h >= 0 if direction == 0 else a + h < A

    def g_arrival(direction, h, k):
        step = 1 if direction == 0 else -1
        place = gg.at[rows_of(a - step * h), cols[k]]
        return remote(
            place, place, gs_sem.at[direction, h, k], gr_sem.at[direction, h, k], "chip",
            c - step * B,
        )

    for k in range(K):
        for direction in range(2):
            @pl.when(g_sends(direction, 1))
            def _():
                g_copy(direction, 1, k).start()

    shared = PODS % 2 == 0
    mate = o + 1 - 2 * (o % 2)
    if shared:
        half = pl.ds(pl.multiple_of((o % 2) * (N // 2), N // 2), N // 2)
    else:
        half = pl.ds(0, N)
    w_copies, m_copies = [], []
    for d in range(1, B):
        t = (b + d) % B
        w_copies.append(remote(
            w_ref.at[:, half], wq.at[shard_of(b), half],
            ws_sem.at[0, d], wr_sem.at[0, d], "chip", a * B + t,
        ))
        if shared:
            came = (b - d + B) % B
            m_copies.append(remote(
                wq.at[shard_of(came), half], wq.at[shard_of(came), half],
                ws_sem.at[1, d], wr_sem.at[1, d], "outer", mate,
            ))
    for cp in w_copies:
        cp.start()

    xg[rows_of(a), :] = x_ref[:, pl.ds(pl.multiple_of(a * Q, Q), Q)]
    gg[rows_of(a), :] = g_ref[...]
    wq[shard_of(b), :] = w_ref[...]
    for cp in x_copies:
        cp.wait_recv()
    xt[...] = xg[...].T

    def y_copy(d, k):
        t = (b + d) % B
        return remote(
            ysend.at[d, :, cols[k]], yrecv.at[d, :, cols[k]],
            ys_sem.at[d, k], yr_sem.at[d, k], "chip", a * B + t,
        )

    def gradient_chunk(k):
        for d in range(1, B):
            t = (b + d) % B
            part = dot(xt[shard_of(t), :], gg[:, cols[k]], 1, 0)
            ysend[d, :, cols[k]] = part.astype(BF16)
            y_copy(d, k).start()
        part = dot(xt[shard_of(b), :], gg[:, cols[k]], 1, 0)
        ne_ref[:, cols[k]] = part

    def o_copy(direction, r, k):
        s_buf, r_buf = (up_s, up_r) if direction == 0 else (dn_s, dn_r)
        return remote(
            s_buf.at[r, :, cols[k]], r_buf.at[r, :, cols[k]],
            rs_sem.at[direction, r, k], rr_sem.at[direction, r, k], "chip",
            c + B if direction == 0 else c - B,
        )

    def o_sends(direction, r):
        return a + r < A if direction == 0 else a - r >= 0

    def o_gets(direction, r):
        if direction == 0:
            return jnp.logical_and(a >= 1, a - 1 + r < A)
        return jnp.logical_and(a + 1 < A, a + 1 - r >= 0)

    def out_stage(r):
        for k in range(K):
            for direction in range(2):
                s_buf, r_buf = (up_s, up_r) if direction == 0 else (dn_s, dn_r)

                @pl.when(o_sends(direction, r))
                def _():
                    token = a + r if direction == 0 else a - r
                    s_buf[r, :, cols[k]] = dot(xg[rows_of(token), :], wq[:, cols[k]], 1, 0).astype(BF16)
                    if r + 1 < A:
                        @pl.when(o_gets(direction, r + 1))
                        def _():
                            o_copy(direction, r + 1, k).wait_recv()
                            s_buf[r, :, cols[k]] = (
                                s_buf[r, :, cols[k]].astype(F32) + r_buf[r + 1, :, cols[k]].astype(F32)
                            ).astype(BF16)
                    o_copy(direction, r, k).start()

    basis = basis_ref[...]

    def merge_chunk(k):
        part = ne_ref[:, cols[k]]
        for d in range(1, B):
            y_copy(d, k).wait_recv()
            part = part + yrecv[d, :, cols[k]].astype(F32)
        part = part / TOK_DEV + err_ref[:, cols[k]]
        ne_ref[:, cols[k]] = part
        return thin_dot(basis[:, k * CN : (k + 1) * CN], part, 1)

    total = jnp.zeros((R, S), F32)
    last = A - 2 + K
    for wave in range(1, last + 1):
        for h in range(1, A):
            k = wave - h
            if 0 <= k < K:
                for direction in range(2):
                    @pl.when(g_gets(direction, h))
                    def _():
                        g_arrival(direction, h, k).wait_recv()
                    if h + 1 < A:
                        @pl.when(g_sends(direction, h + 1))
                        def _():
                            g_copy(direction, h + 1, k).start()
        k = wave - (A - 1)
        if 0 <= k < K:
            gradient_chunk(k)
            if k >= 1:
                total = total + merge_chunk(k - 1)
        if wave == 2:
            for cp in w_copies:
                cp.wait_recv()
            for cp in m_copies:
                cp.start()
        if wave == 3:
            for cp in m_copies:
                cp.wait_recv()
            out_stage(A - 1)
        if wave == last - 1:
            for r in range(A - 2, 1, -1):
                out_stage(r)
    total = total + merge_chunk(K - 1)
    left_s[...] = total
    l_copies = [
        remote(left_s, left_r.at[d], ls_sem.at[d], lr_sem.at[d], "outer", (o + d) % PODS)
        for d in range(1, PODS)
    ]
    for cp in l_copies:
        cp.start()
    out_stage(1)
    for d, cp in enumerate(l_copies):
        cp.wait_recv()
        total = total + left_r[d + 1]
    left = orthonormal(total / PODS)

    f_peers = [(c + d) % NC for d in range(1, NC)]
    fl[0] = left
    fl_copies = [
        remote(fl.at[0], fl.at[d + 1], fs_sem.at[0, d], fq_sem.at[0, d], "chip", t)
        for d, t in enumerate(f_peers)
    ]
    right = thin_dot(left, ne_ref[...], 0).astype(BF16)
    right_s[...] = right
    h_copies = [
        remote(right_s, right_r.at[d], hs_sem.at[d], hr_sem.at[d], "outer", (o + d) % PODS)
        for d in range(1, PODS)
    ]
    for cp in h_copies:
        cp.start()
    for cp in fl_copies:
        cp.start()
    for k in range(K):
        own[:, cols[k]] = dot(xg[rows_of(a), :], wq[:, cols[k]], 1, 0)
    right = right.astype(F32)
    for d, cp in enumerate(h_copies):
        cp.wait_recv()
        right = right + right_r[d + 1].astype(F32)
    right = right / PODS
    fr[0] = right.astype(BF16)
    fr_copies = [
        remote(fr.at[0], fr.at[d + 1], fs_sem.at[1, d], fq_sem.at[1, d], "chip", t)
        for d, t in enumerate(f_peers)
    ]
    for cp in fr_copies:
        cp.start()
    left_high, left_low = halves(left)
    right_high, right_low = halves(right)
    lefts = stack(left_high, left_low, left_high)
    rights = stack(right_high, right_high, right_low)
    for k in range(K):
        ne_ref[:, cols[k]] = ne_ref[:, cols[k]] - dot(
            lefts, rights[:, k * CN : (k + 1) * CN], 0, 0
        )

    z_rows = []
    for d in range(NC):
        if d > 0:
            fl_copies[d - 1].wait_recv()
        owner = (c - d + NC) % NC
        both = dot(stack(*halves(fl[d])), x_ref[:, shard_of(owner)], 1, 1)
        z_rows.append(both[:R] + both[R:])
    z = stack(*halves(jnp.concatenate(z_rows, axis=0)))
    for cp in fr_copies:
        cp.wait_recv()
    for k in range(K):
        rights = jnp.concatenate([fr[d, :, cols[k]].astype(F32) for d in range(NC)], axis=0)
        delta = dot(z, stack(rights, rights), 0, 0)
        for direction in range(2):
            r_buf = up_r if direction == 0 else dn_r

            @pl.when(o_gets(direction, 1))
            def _():
                o_copy(direction, 1, k).wait_recv()

            @pl.when(jnp.logical_not(o_gets(direction, 1)))
            def _():
                r_buf[1, :, cols[k]] = jnp.zeros((T, CN), BF16)
        mine = own[:, cols[k]] + up_r[1, :, cols[k]].astype(F32) + dn_r[1, :, cols[k]].astype(F32)
        out_ref[:, cols[k]] = (mine - LEARNING_RATE * delta).astype(BF16)

    for cp in x_copies + w_copies + m_copies + l_copies + h_copies + fl_copies + fr_copies:
        cp.wait_send()
    for k in range(K):
        for d in range(1, B):
            y_copy(d, k).wait_send()
        for direction in range(2):
            for h in range(1, A):
                @pl.when(g_sends(direction, h))
                def _():
                    g_copy(direction, h, k).wait_send()

                @pl.when(o_sends(direction, h))
                def _():
                    o_copy(direction, h, k).wait_send()


def shards(inputs, out_grads, weight, start_basis, error_buffer):
    PODS, NC = lax.axis_size("outer"), lax.axis_size("chip")
    A = 4 if NC % 4 == 0 else NC
    B = NC // A
    T, D = inputs.shape
    N = out_grads.shape[1]
    S = weight.shape[0]
    R = start_basis.shape[0]
    Q = B * S
    K = CHUNKS
    dma = pltpu.SemaphoreType.DMA
    vmem = pl.BlockSpec(memory_space=pltpu.VMEM)
    outputs, new_error = pl.pallas_call(
        functools.partial(kernel, A, B, PODS),
        out_shape=(
            jax.ShapeDtypeStruct((T, N), BF16),
            jax.ShapeDtypeStruct((S, N), F32),
        ),
        in_specs=[vmem] * 5,
        out_specs=(vmem, vmem),
        scratch_shapes=[
            pltpu.VMEM((A * T, Q), BF16),
            pltpu.VMEM((Q, A * T), BF16),
            pltpu.VMEM((A * T, N), BF16),
            pltpu.VMEM((Q, N), BF16),
            pltpu.VMEM((B, S, N), BF16),
            pltpu.VMEM((B, S, N), BF16),
            pltpu.VMEM((A, T, N), BF16),
            pltpu.VMEM((A, T, N), BF16),
            pltpu.VMEM((A, T, N), BF16),
            pltpu.VMEM((A, T, N), BF16),
            pltpu.VMEM((R, S), F32),
            pltpu.VMEM((PODS, R, S), F32),
            pltpu.VMEM((R, N), BF16),
            pltpu.VMEM((PODS, R, N), BF16),
            pltpu.VMEM((NC, R, S), F32),
            pltpu.VMEM((NC, R, N), BF16),
            pltpu.VMEM((T, N), F32),
            dma((A,)), dma((A,)), dma((2, B)), dma((2, B)),
            dma((2, A, K)), dma((2, A, K)), dma((B, K)), dma((B, K)),
            dma((2, A, K)), dma((2, A, K)),
            dma((PODS,)), dma((PODS,)), dma((PODS,)), dma((PODS,)),
            dma((2, NC)), dma((2, NC)),
        ],
        compiler_params=pltpu.CompilerParams(
            collective_id=0, has_side_effects=True, vmem_limit_bytes=56 * 1024 * 1024
        ),
        name="step",
    )(inputs, out_grads, weight, start_basis, error_buffer[0])
    return outputs, new_error[None]


def solution(mesh):
    return jax.shard_map(
        shards,
        mesh=mesh,
        in_specs=(
            P(("outer", "chip"), None),
            P(("outer", "chip"), None),
            P("chip", None),
            P("chip", None),
            P("outer", "chip", None),
        ),
        out_specs=(P(("outer", "chip"), None), P("outer", "chip", None)),
        check_vma=False,
    )
```

profile of v0, /device:TPU:0, one launch (start us, length us, event | category | flops | bytes accessed | tf_op | source)
XLA Modules:
  0.0 90.1 jit_solution(835630917622915969)
XLA Ops:
  0.6 84.5 %step.1 = (bf16[128,2048]{1,0:T(8,128)(2,1)}, f32[256,2048]{1,0:T(8,128)}) custom-call(bf16[128,2048]{1,0:T(8,128)(2,1)} %x_ref.1, bf16[128,2048]{1,0:T(8,128)(2,1)} %g_ref.1, bf16[256,2048]{1,0:T(8,128)(2,1)} %w_ref.1, f32[8,2048]{1,0:T(8,128)} %basis_ref.1, f32[256,2048]{1,0:T(8,128)} %bitcast.2), custom_call_target="tpu_custom_call" | custom-call | tf_op jit(solution)/shard_map/step/pallas_call | solution.py:368
  85.1 1.9 %copy.9 = bf16[128,2048]{1,0:T(8,128)(2,1)} copy(bf16[128,2048]{1,0:T(8,128)(2,1)} %get-tuple-element.8) | data formatting | bytes 1048576
  87.0 3.1 %copy.10 = f32[1,256,2048]{2,1,0:T(8,128)} copy(f32[1,256,2048]{2,1,0:T(8,128)} %bitcast.3) | data formatting | bytes 4194304
where the time goes:
time: 90.3 us; the launch traced here: 90.1 us
  Pallas kernels  84.5 us (94%)
  local copies, waits for them, and re-layouts  5.02 us (6%)
    pallas_call x1, Pallas kernels, shards(): pl.pallas_call(functools.partial(kernel, A, B, PODS), out_shape=(jax.Shap...  84.5 us
    unnamed x2, local copies, waits for them, and re-layouts  5.02 us

commit v1 on v0

v1 whole, which is shorter than its diff:
```python
import functools

import jax
import jax.numpy as jnp
from jax import lax
from jax.experimental import pallas as pl
from jax.experimental.pallas import tpu as pltpu
from jax.sharding import PartitionSpec as P

TOK_DEV = 128
LEARNING_RATE = 0.2
CHUNKS = 4
HELD = 2
F32 = jnp.float32
BF16 = jnp.bfloat16


def dot(a, b, ca, cb):
    return lax.dot_general(
        a, b, (((ca,), (cb,)), ((), ())), preferred_element_type=F32
    )


def halves(v):
    high = v.astype(BF16).astype(F32)
    return high, v - high


def stack(*parts):
    return jnp.concatenate(parts, axis=0).astype(BF16)


def split(thin):
    return stack(*halves(thin))


def fold(both):
    n = both.shape[0] // 2
    return both[:n] + both[n:]


def thin_dot(thin, wide_high, wide_low, cb):
    n = thin.shape[0]
    both = split(thin)
    return fold(dot(both, wide_high, 1, cb)) + dot(both[:n], wide_low, 1, cb)


def orthonormal(v):
    count = v.shape[0]
    row = lax.broadcasted_iota(jnp.int32, (count, 1), 0)
    for k in range(count):
        pivot = v[k : k + 1, :]
        d = jnp.sum(v * pivot, axis=1, keepdims=True)
        norm = d[k : k + 1, :] + 1.0
        scale = jnp.where(row > k, d / norm, 0.0)
        unit = pivot / jnp.sqrt(norm)
        v = jnp.where(row == k, unit, v - scale * pivot)
    return v


def kernel(
    A, B, PODS,
    x_hbm, g_hbm, w_hbm, basis_hbm, err_hbm,
    out_ref, ne_ref,
    xv, xg, xt, gg, wq, bas, ev, eh, el, ysend, yrecv, up_s, up_r, dn_s, dn_r,
    left_s, left_r, zs, zr, rp, rq, rz, rown, rall, own,
    in_sem, xs_sem, xr_sem, ws_sem, wr_sem, bs_sem, br_sem, gs_sem, gr_sem, ys_sem, yr_sem,
    rs_sem, rr_sem, ls_sem, lr_sem, zs_sem, zr_sem, hs_sem, hr_sem, ps_sem, pr_sem,
    as_sem, ar_sem, fs_sem, fr_sem,
):
    o = lax.axis_index("outer")
    c = lax.axis_index("chip")
    a, b = c // B, c % B
    T = x_hbm.shape[0]
    S, N = w_hbm.shape
    Q = B * S
    R = basis_hbm.shape[0]
    K = CHUNKS
    CN = N // K
    NP = N // PODS
    cols = [pl.ds(k * CN, CN) for k in range(K)]

    def rows_of(s):
        return pl.ds(pl.multiple_of(s * T, T), T)

    def shard_of(s):
        return pl.ds(pl.multiple_of(s * S, S), S)

    def share_of(s):
        return pl.ds(pl.multiple_of(s * NP, NP), NP)

    ins = [
        pltpu.make_async_copy(src, dst, in_sem.at[i])
        for i, (src, dst) in enumerate([
            (x_hbm, xv),
            (basis_hbm, bas.at[0]),
            (w_hbm, wq.at[shard_of(b)]),
            (g_hbm, gg.at[rows_of(a)]),
            (x_hbm.at[:, pl.ds(pl.multiple_of(a * Q, Q), Q)], xg.at[rows_of(a)]),
            (err_hbm, ev),
        ])
    ]
    for cp in ins:
        cp.start()

    line = [((a + d) % A) * B + b for d in range(1, A)]
    group = [(do, db) for do in range(PODS) for db in range(B) if do or db]

    def member(do, db):
        return {"outer": (o + do) % PODS, "chip": a * B + (b + db) % B}

    def remote(src, dst, ss, rs, where):
        return pltpu.make_async_remote_copy(
            src_ref=src, dst_ref=dst, send_sem=ss, recv_sem=rs,
            device_id=where, device_id_type=pl.DeviceIdType.MESH,
        )

    barrier = pltpu.get_barrier_semaphore()
    for t in line:
        pl.semaphore_signal(
            barrier, inc=1, device_id={"chip": t}, device_id_type=pl.DeviceIdType.MESH
        )
    for do, db in group:
        pl.semaphore_signal(
            barrier, inc=1, device_id=member(do, db), device_id_type=pl.DeviceIdType.MESH
        )
    pl.semaphore_wait(barrier, len(line) + len(group))

    x_copies = []
    for d in range(1, A):
        t = (a + d) % A
        x_copies.append(remote(
            xv.at[:, pl.ds(pl.multiple_of(t * Q, Q), Q)], xg.at[rows_of(a)],
            xs_sem.at[d], xr_sem.at[d], {"chip": t * B + b},
        ))
    b_copies = [
        remote(bas.at[0], bas.at[(-d) % B], bs_sem.at[d], br_sem.at[d], member(0, d))
        for d in range(1, B)
    ]

    def g_copy(direction, h, k):
        step = 1 if direction == 0 else -1
        source = a - step * (h - 1)
        place = gg.at[rows_of(source), cols[k]]
        return remote(
            place, place, gs_sem.at[direction, h, k], gr_sem.at[direction, h, k],
            {"chip": c + step * B},
        )

    def g_sends(direction, h):
        return (
            jnp.logical_and(a - (h - 1) >= 0, a + 1 < A)
            if direction == 0
            else jnp.logical_and(a + (h - 1) < A, a >= 1)
        )

    def g_gets(direction, h):
        return a - h >= 0 if direction == 0 else a + h < A

    def g_arrival(direction, h, k):
        step = 1 if direction == 0 else -1
        place = gg.at[rows_of(a - step * h), cols[k]]
        return remote(
            place, place, gs_sem.at[direction, h, k], gr_sem.at[direction, h, k],
            {"chip": c - step * B},
        )

    shared = PODS % 2 == 0
    mate = o + 1 - 2 * (o % 2)
    if shared:
        half = pl.ds(pl.multiple_of((o % 2) * (N // 2), N // 2), N // 2)
    else:
        half = pl.ds(0, N)
    w_copies, m_copies = [], []
    for d in range(1, B):
        w_copies.append(remote(
            wq.at[shard_of(b), half], wq.at[shard_of(b), half],
            ws_sem.at[0, d], wr_sem.at[0, d], member(0, d),
        ))
        if shared:
            came = (b - d + B) % B
            m_copies.append(remote(
                wq.at[shard_of(came), half], wq.at[shard_of(came), half],
                ws_sem.at[1, d], wr_sem.at[1, d], {"outer": mate},
            ))

    ins[0].wait()
    for cp in x_copies:
        cp.start()
    ins[1].wait()
    for cp in b_copies:
        cp.start()
    ins[2].wait()
    for cp in w_copies:
        cp.start()
    ins[3].wait()
    for k in range(K):
        for direction in range(2):
            @pl.when(g_sends(direction, 1))
            def _():
                g_copy(direction, 1, k).start()
    ins[4].wait()
    ins[5].wait()

    for k in range(K):
        high, low = halves(ev[:, cols[k]])
        eh[:, cols[k]] = high.astype(BF16)
        el[:, cols[k]] = low.astype(BF16)
    fed = thin_dot(bas[0], eh[...], el[...], 1)

    for cp in x_copies:
        cp.wait_recv()
    xt[...] = xg[...].T
    for cp in b_copies:
        cp.wait_recv()
    for cp in w_copies:
        cp.wait_recv()
    for cp in m_copies:
        cp.start()

    def y_copy(d, k):
        return remote(
            ysend.at[d - 1, :, cols[k]], yrecv.at[d - 1, :, cols[k]],
            ys_sem.at[d, k], yr_sem.at[d, k], member(0, d),
        )

    def gradient_chunk(k):
        for d in range(1, B):
            part = dot(xt[shard_of((b + d) % B), :], gg[:, cols[k]], 1, 0)
            ysend[d - 1, :, cols[k]] = part.astype(BF16)
            y_copy(d, k).start()
        ne_ref[:, cols[k]] = dot(xt[shard_of(b), :], gg[:, cols[k]], 1, 0)

    def merge_chunk(k):
        part = ne_ref[:, cols[k]]
        for d in range(1, B):
            y_copy(d, k).wait_recv()
            part = part + yrecv[d - 1, :, cols[k]].astype(F32)
        ne_ref[:, cols[k]] = part / TOK_DEV + ev[:, cols[k]]

    def project_chunk(k):
        basis = split(jnp.concatenate([bas[d, :, cols[k]] for d in range(B)], axis=0))
        return fold(dot(basis, gg[:, cols[k]], 1, 1))

    def o_copy(direction, r, k):
        s_buf, r_buf = (up_s, up_r) if direction == 0 else (dn_s, dn_r)
        return remote(
            s_buf.at[r - 1, :, cols[k]], r_buf.at[r - 1, :, cols[k]],
            rs_sem.at[direction, r, k], rr_sem.at[direction, r, k],
            {"chip": c + B if direction == 0 else c - B},
        )

    def o_first(direction):
        return a == 0 if direction == 0 else a == A - 1

    def o_sends(direction, r):
        return a + r < A if direction == 0 else a - r >= 0

    def o_gets(direction, r):
        if direction == 0:
            return jnp.logical_and(a >= 1, a - 1 + r < A)
        return jnp.logical_and(a + 1 < A, a + 1 - r >= 0)

    def out_piece(direction, r, k, first):
        s_buf, r_buf = (up_s, up_r) if direction == 0 else (dn_s, dn_r)
        leads = o_first(direction)
        if not first:
            leads = jnp.logical_not(leads)

        @pl.when(jnp.logical_and(o_sends(direction, r), leads))
        def _():
            token = a + r if direction == 0 else a - r
            part = dot(xg[rows_of(token), :], wq[:, cols[k]], 1, 0)
            if not first:
                o_copy(direction, r + 1, k).wait_recv()
                part = part + r_buf[r, :, cols[k]].astype(F32)
            s_buf[r - 1, :, cols[k]] = part.astype(BF16)
            o_copy(direction, r, k).start()

    def out_pieces(r, ks, first):
        for k in ks:
            for direction in range(2):
                out_piece(direction, r, k, first)

    early, held = range(K - HELD), range(K - HELD, K)
    l_copies = [
        remote(left_s, left_r.at[j], ls_sem.at[j], lr_sem.at[j], member(do, db))
        for j, (do, db) in enumerate(group)
    ]
    thin = jnp.zeros((B * R, A * T), F32)
    last = A - 2 + K
    for wave in range(1, last + 1):
        for h in range(1, A):
            k = wave - h
            if 0 <= k < K:
                for direction in range(2):
                    @pl.when(g_gets(direction, h))
                    def _():
                        g_arrival(direction, h, k).wait_recv()
                    if h + 1 < A:
                        @pl.when(g_sends(direction, h + 1))
                        def _():
                            g_copy(direction, h + 1, k).start()
        if wave == 1:
            for cp in m_copies:
                cp.wait_recv()
            for r in range(A - 1, 1, -1):
                out_pieces(r, range(K), True)
            out_pieces(1, early, True)
            for k in range(K):
                own[:, cols[k]] = dot(xg[rows_of(a), :], wq[:, cols[k]], 1, 0)
        k = wave - (A - 1)
        if 0 <= k < K:
            thin = thin + project_chunk(k)
            if k == K - 1:
                for d in range(B):
                    mine = thin[d * R : (d + 1) * R, :]
                    part = fold(dot(split(mine), xg[:, shard_of((b + d) % B)], 1, 0)) / TOK_DEV
                    left_s[d] = part + fed if d == 0 else part
                for cp in l_copies:
                    cp.start()
            gradient_chunk(k)
            if k >= 1:
                merge_chunk(k - 1)
    for r in range(A - 2, 1, -1):
        out_pieces(r, range(K), False)

    total = [left_s[d] for d in range(B)]
    for j, (do, db) in enumerate(group):
        l_copies[j].wait_recv()
        for d in range(B):
            total[d] = total[d] + left_r[j, (d + db) % B]
    left = [orthonormal(total[d] / PODS) for d in range(B)]

    z = jnp.concatenate(
        [fold(dot(split(left[d]), xt[shard_of((b + d) % B), :], 1, 0)) for d in range(B)], axis=0
    )
    for t in range(A):
        zs[t] = z[:, t * T : (t + 1) * T]
    z_copies = []
    for d in range(1, A):
        t = (a + d) % A
        z_copies.append(remote(
            zs.at[t], zr.at[a], zs_sem.at[d], zr_sem.at[d], {"chip": t * B + b}
        ))
    z_pair = split(z)
    for k in range(K):
        part = fold(dot(z_pair, gg[:, cols[k]], 1, 0)) / TOK_DEV
        lead = part[:R] + thin_dot(left[0], eh[:, cols[k]], el[:, cols[k]], 0)
        rp[0, :, cols[k]] = lead.astype(BF16)
        for d in range(1, B):
            rp[d, :, cols[k]] = part[d * R : (d + 1) * R].astype(BF16)
    h_copies = [
        remote(
            rp.at[db, :, share_of((o + do) % PODS)], rq.at[j],
            hs_sem.at[j], hr_sem.at[j], member(do, db),
        )
        for j, (do, db) in enumerate(group)
    ]
    for cp in h_copies:
        cp.start()
    for cp in z_copies:
        cp.start()
    zr[a] = zs[a]
    out_pieces(1, early, False)

    right = rp[0, :, share_of(o)].astype(F32)
    for j, cp in enumerate(h_copies):
        cp.wait_recv()
        right = right + rq[j].astype(F32)
    rz[a] = (right / PODS).astype(BF16)
    p_copies = [
        remote(
            rz.at[a], rown.at[:, share_of(o)], ps_sem.at[do], pr_sem.at[do], member(do, 0)
        )
        for do in range(1, PODS)
    ]
    a_copies = [
        remote(rz.at[a], rz.at[a], as_sem.at[d + 1], ar_sem.at[d + 1], {"chip": t})
        for d, t in enumerate(line)
    ]
    for cp in a_copies + p_copies:
        cp.start()
    rown[:, share_of(o)] = rz[a]
    for first in (True, False):
        out_pieces(1, held, first)
    merge_chunk(K - 1)

    for cp in a_copies:
        cp.wait_recv()
    f_copies = [
        remote(
            rz, rall.at[(-db) % B, :, :, share_of(o)], fs_sem.at[j], fr_sem.at[j], member(do, db)
        )
        for j, (do, db) in enumerate(group)
    ]
    for cp in f_copies:
        cp.start()
    rall[0, :, :, share_of(o)] = rz[...]
    for cp in p_copies:
        cp.wait_recv()
    lefts = split(left[0])
    for k in range(K):
        mine = rown[:, cols[k]].astype(F32)
        ne_ref[:, cols[k]] = ne_ref[:, cols[k]] - dot(lefts, stack(mine, mine), 0, 0)

    for cp in z_copies:
        cp.wait_recv()
    z = split(jnp.concatenate(
        [zr[t, d * R : (d + 1) * R, :] for d in range(B) for t in range(A)], axis=0
    ))
    for cp in f_copies:
        cp.wait_recv()
    for k in range(K):
        rights = jnp.concatenate(
            [rall[d, t, :, cols[k]].astype(F32) for d in range(B) for t in range(A)], axis=0
        )
        delta = dot(z, stack(rights, rights), 0, 0)
        for direction in range(2):
            r_buf = up_r if direction == 0 else dn_r

            @pl.when(o_gets(direction, 1))
            def _():
                o_copy(direction, 1, k).wait_recv()

            @pl.when(jnp.logical_not(o_gets(direction, 1)))
            def _():
                r_buf[0, :, cols[k]] = jnp.zeros((T, CN), BF16)
        mine = own[:, cols[k]] + up_r[0, :, cols[k]].astype(F32) + dn_r[0, :, cols[k]].astype(F32)
        out_ref[:, cols[k]] = (mine - LEARNING_RATE * delta).astype(BF16)

    for cp in x_copies + b_copies + w_copies + m_copies + l_copies + z_copies + h_copies:
        cp.wait_send()
    for cp in p_copies + a_copies + f_copies:
        cp.wait_send()
    for k in range(K):
        for d in range(1, B):
            y_copy(d, k).wait_send()
        for direction in range(2):
            for h in range(1, A):
                @pl.when(g_sends(direction, h))
                def _():
                    g_copy(direction, h, k).wait_send()

                @pl.when(o_sends(direction, h))
                def _():
                    o_copy(direction, h, k).wait_send()


def shards(inputs, out_grads, weight, start_basis, error_buffer):
    PODS, NC = lax.axis_size("outer"), lax.axis_size("chip")
    A = 4 if NC % 4 == 0 else NC
    B = NC // A
    T, D = inputs.shape
    N = out_grads.shape[1]
    S = weight.shape[0]
    R = start_basis.shape[0]
    Q = B * S
    K = CHUNKS
    G = PODS * B
    dma = pltpu.SemaphoreType.DMA
    vmem = pl.BlockSpec(memory_space=pltpu.VMEM)
    hbm = pl.BlockSpec(memory_space=pltpu.HBM)
    outputs, new_error = pl.pallas_call(
        functools.partial(kernel, A, B, PODS),
        out_shape=(
            jax.ShapeDtypeStruct((T, N), BF16),
            jax.ShapeDtypeStruct((S, N), F32),
        ),
        in_specs=[hbm] * 5,
        out_specs=(vmem, vmem),
        scratch_shapes=[
            pltpu.VMEM((T, D), BF16),
            pltpu.VMEM((A * T, Q), BF16),
            pltpu.VMEM((Q, A * T), BF16),
            pltpu.VMEM((A * T, N), BF16),
            pltpu.VMEM((Q, N), BF16),
            pltpu.VMEM((B, R, N), F32),
            pltpu.VMEM((S, N), F32),
            pltpu.VMEM((S, N), BF16),
            pltpu.VMEM((S, N), BF16),
            pltpu.VMEM((B - 1, S, N), BF16),
            pltpu.VMEM((B - 1, S, N), BF16),
            pltpu.VMEM((A - 1, T, N), BF16),
            pltpu.VMEM((A - 1, T, N), BF16),
            pltpu.VMEM((A - 1, T, N), BF16),
            pltpu.VMEM((A - 1, T, N), BF16),
            pltpu.VMEM((B, R, S), F32),
            pltpu.VMEM((G - 1, B, R, S), F32),
            pltpu.VMEM((A, B * R, T), F32),
            pltpu.VMEM((A, B * R, T), F32),
            pltpu.VMEM((B, R, N), BF16),
            pltpu.VMEM((G - 1, R, N // PODS), BF16),
            pltpu.VMEM((A, R, N // PODS), BF16),
            pltpu.VMEM((R, N), BF16),
            pltpu.VMEM((B, A, R, N), BF16),
            pltpu.VMEM((T, N), F32),
            dma((6,)), dma((A,)), dma((A,)), dma((2, B)), dma((2, B)), dma((B,)), dma((B,)),
            dma((2, A, K)), dma((2, A, K)), dma((B, K)), dma((B, K)),
            dma((2, A, K)), dma((2, A, K)),
            dma((G,)), dma((G,)), dma((A,)), dma((A,)), dma((G,)), dma((G,)),
            dma((PODS,)), dma((PODS,)), dma((A,)), dma((A,)), dma((G,)), dma((G,)),
        ],
        compiler_params=pltpu.CompilerParams(
            collective_id=0, has_side_effects=True, vmem_limit_bytes=40 * 1024 * 1024
        ),
        name="step",
    )(inputs, out_grads, weight, start_basis, error_buffer[0])
    return outputs, new_error[None]


def solution(mesh):
    return jax.shard_map(
        shards,
        mesh=mesh,
        in_specs=(
            P(("outer", "chip"), None),
            P(("outer", "chip"), None),
            P("chip", None),
            P("chip", None),
            P("outer", "chip", None),
        ),
        out_specs=(P(("outer", "chip"), None), P("outer", "chip", None)),
        check_vma=False,
    )
```

time: 90.3 us -> 91.4 us (1.012)
  local copies, waits for them, and re-layouts: 5.02 us -> 7.84 us
  Pallas kernels: 84.5 us -> 82.6 us
    unnamed x2 -> x12, local copies, waits for them, and re-layouts: 5.02 us -> 7.84 us
    pallas_call x1, Pallas kernels: 84.5 us -> 82.6 us  [shards(): pl.pallas_call(functools.partial(kernel, A, B, PODS), out_shape=(jax.Shap...]
where the time goes in v1:
time: 91.4 us; the launch traced here: 91.1 us
  Pallas kernels  82.6 us (90%)
  local copies, waits for them, and re-layouts  7.84 us (9%)
    pallas_call x1, Pallas kernels, shards(): pl.pallas_call(functools.partial(kernel, A, B, PODS), out_shape=(jax.Shap...  82.6 us
    unnamed x12, local copies, waits for them, and re-layouts  7.84 us

profile of v1, /device:TPU:0, one launch (start us, length us, event | category | flops | bytes accessed | tf_op | source)
XLA Modules:
  0.0 91.1 jit_solution(12887486411848295285)
XLA Ops:
  0.6 0.0 copy-start
  0.6 1.6 %copy-done = f32[1,256,2048]{2,1,0:T(8,128)S(1)} copy-done((f32[1,256,2048]{2,1,0:T(8,128)S(1)}, f32[1,256,2048]{2,1,0:T(8,128)}, u32[]{:S(2)}) %copy-start) | copy-done | bytes 2097176
  2.2 0.0 copy-start.1
  2.2 1.2 %copy-done.1 = bf16[256,2048]{1,0:T(8,128)(2,1)S(1)} copy-done((bf16[256,2048]{1,0:T(8,128)(2,1)S(1)}, bf16[256,2048]{1,0:T(8,128)(2,1)}, u32[]{:S(2)}) %copy-start.1) | copy-done | bytes 1048600
  3.4 0.0 copy-start.2
  3.5 1.0 %copy-done.2 = bf16[128,2048]{1,0:T(8,128)(2,1)S(1)} copy-done((bf16[128,2048]{1,0:T(8,128)(2,1)S(1)}, bf16[128,2048]{1,0:T(8,128)(2,1)}, u32[]{:S(2)}) %copy-start.2) | copy-done | bytes 524312
  4.5 0.0 copy-start.3
  4.5 1.0 %copy-done.3 = bf16[128,2048]{1,0:T(8,128)(2,1)S(1)} copy-done((bf16[128,2048]{1,0:T(8,128)(2,1)S(1)}, bf16[128,2048]{1,0:T(8,128)(2,1)}, u32[]{:S(2)}) %copy-start.3) | copy-done | bytes 524312
  5.5 0.0 copy-start.4
  5.5 0.8 copy-done.4
  6.4 82.6 %step.1 = (bf16[128,2048]{1,0:T(8,128)(2,1)S(1)}, f32[256,2048]{1,0:T(8,128)S(1)}) custom-call(bf16[128,2048]{1,0:T(8,128)(2,1)S(1)} %copy-done.2, bf16[128,2048]{1,0:T(8,128)(2,1)S(1)} %copy-done.3, bf16[256,2048]{1,0:T(8,128)(2,1)S(1)} %copy-done.1, f32[8,2048]{1,0:T(8,128)S(1)} %copy-done.4, f32[256,2048]{1,0:T(8,128)S(1)} %bitcast.2), custom_call_target="tpu_custom_call" | custom-call | tf_op jit(solution)/shard_map/step/pallas_call | solution.py:464
  89.0 0.8 copy.9
  89.8 1.3 %copy.10 = f32[1,256,2048]{2,1,0:T(8,128)} copy(f32[1,256,2048]{2,1,0:T(8,128)S(1)} %bitcast.3) | data formatting | bytes 4194304
Async XLA Ops:
  0.6 1.6 %copy-start = (f32[1,256,2048]{2,1,0:T(8,128)S(1)}, f32[1,256,2048]{2,1,0:T(8,128)}, u32[]{:S(2)}) copy-start(f32[1,256,2048]{2,1,0:T(8,128)} %param.9) | copy-start | bytes 6291460
  2.2 1.2 %copy-start.1 = (bf16[256,2048]{1,0:T(8,128)(2,1)S(1)}, bf16[256,2048]{1,0:T(8,128)(2,1)}, u32[]{:S(2)}) copy-start(bf16[256,2048]{1,0:T(8,128)(2,1)} %w_hbm.1) | copy-start | bytes 3145732
  3.4 1.0 %copy-start.2 = (bf16[128,2048]{1,0:T(8,128)(2,1)S(1)}, bf16[128,2048]{1,0:T(8,128)(2,1)}, u32[]{:S(2)}) copy-start(bf16[128,2048]{1,0:T(8,128)(2,1)} %x_hbm.1) | copy-start | bytes 1572868
  4.5 1.0 %copy-start.3 = (bf16[128,2048]{1,0:T(8,128)(2,1)S(1)}, bf16[128,2048]{1,0:T(8,128)(2,1)}, u32[]{:S(2)}) copy-start(bf16[128,2048]{1,0:T(8,128)(2,1)} %g_hbm.1) | copy-start | bytes 1572868
  5.5 0.8 copy-start.4

commit v2 on v1

--- a/solution.py
+++ b/solution.py
@@ -9,8 +9,9 @@
 
 TOK_DEV = 128
 LEARNING_RATE = 0.2
-CHUNKS = 4
-HELD = 2
+CHUNKS = 8
+AHEAD = 4
+PIECES = 2
 F32 = jnp.float32
 BF16 = jnp.bfloat16
 
@@ -58,15 +59,43 @@
     return v
 
 
+def plan_of(A, K):
+    firsts = [("first", r, k) for r in range(A - 1, 0, -1) for k in range(K)]
+    rests = [("rest", r, k) for r in range(A - 2, 0, -1) for k in range(K)]
+
+    def take(queue, count):
+        taken = queue[:count]
+        del queue[:count]
+        return taken
+
+    last = A - 2 + K
+    chain = {
+        2: ["weights", "mates"], 3: ["left1"], 5: ["left2", "own"], last - 3: ["right1"],
+        last - 2: ["right2"], last - 1: ["right3"],
+    }
+    steps = []
+    for wave in range(1, last + 1):
+        steps.append(("wave", wave))
+        if wave == last - 2:
+            steps += take(rests, 3)
+        steps += [(name,) for name in chain.get(wave, [])]
+        if wave >= 3:
+            steps += take(firsts, A - 1)
+        if wave >= last - 3:
+            steps += take(rests, 3)
+    steps += [("right4",)] + firsts + rests
+    return steps + [("merge", k) for k in range(K)]
+
+
 def kernel(
     A, B, PODS,
     x_hbm, g_hbm, w_hbm, basis_hbm, err_hbm,
     out_ref, ne_ref,
-    xv, xg, xt, gg, wq, bas, ev, eh, el, ysend, yrecv, up_s, up_r, dn_s, dn_r,
-    left_s, left_r, zs, zr, rp, rq, rz, rown, rall, own,
-    in_sem, xs_sem, xr_sem, ws_sem, wr_sem, bs_sem, br_sem, gs_sem, gr_sem, ys_sem, yr_sem,
-    rs_sem, rr_sem, ls_sem, lr_sem, zs_sem, zr_sem, hs_sem, hr_sem, ps_sem, pr_sem,
-    as_sem, ar_sem, fs_sem, fr_sem,
+    xv, xg, xt, gg, wq, bas, bz, ball, ev, eh, el, ysend, yrecv, up_s, up_r, dn_s, dn_r,
+    ls, lz, left_s, left_r, zs, zr, rp, rq, rs, rw, rz, rown, rall, own,
+    in_sem, xs_sem, xr_sem, ws_sem, wr_sem, cs_sem, cr_sem, vs_sem, vr_sem, bs_sem, br_sem,
+    gs_sem, gr_sem, ys_sem, yr_sem, rs_sem, rr_sem, js_sem, jr_sem, ls_sem, lr_sem, zs_sem, zr_sem,
+    hs_sem, hr_sem, ts_sem, tr_sem, ps_sem, pr_sem, as_sem, ar_sem, fs_sem, fr_sem,
 ):
     o = lax.axis_index("outer")
     c = lax.axis_index("chip")
@@ -92,10 +121,11 @@
     ins = [
         pltpu.make_async_copy(src, dst, in_sem.at[i])
         for i, (src, dst) in enumerate([
+            (basis_hbm.at[:, share_of(o)], bz.at[a]),
             (x_hbm, xv),
-            (basis_hbm, bas.at[0]),
+            (g_hbm, gg.at[rows_of(a)]),
             (w_hbm, wq.at[shard_of(b)]),
-            (g_hbm, gg.at[rows_of(a)]),
+            (basis_hbm, bas),
             (x_hbm.at[:, pl.ds(pl.multiple_of(a * Q, Q), Q)], xg.at[rows_of(a)]),
             (err_hbm, ev),
         ])
@@ -133,8 +163,32 @@
             xv.at[:, pl.ds(pl.multiple_of(t * Q, Q), Q)], xg.at[rows_of(a)],
             xs_sem.at[d], xr_sem.at[d], {"chip": t * B + b},
         ))
+    def along(src, dst, ss, rs):
+        return [
+            remote(src((a + d) % A), dst, ss.at[d], rs.at[d], {"chip": ((a + d) % A) * B + b})
+            for d in range(1, A)
+        ]
+
+    def across(src, dst, ss, rs):
+        return [
+            remote(src(do, db), dst(j, db), ss.at[j], rs.at[j], member(do, db))
+            for j, (do, db) in enumerate(group)
+        ]
+
+    c_copies = along(lambda t: bz.at[a], bz.at[a], cs_sem, cr_sem)
     b_copies = [
-        remote(bas.at[0], bas.at[(-d) % B], bs_sem.at[d], br_sem.at[d], member(0, d))
+        [
+            remote(
+                bz if d == 0 else ball.at[d, :, :, share_of(o)],
+                ball.at[d, :, :, share_of(o)],
+                bs_sem.at[d, do], br_sem.at[d, do], member(do, 0),
+            )
+            for do in range(1, PODS)
+        ]
+        for d in range(B)
+    ]
+    v_copies = [
+        remote(bz, ball.at[(-d) % B, :, :, share_of(o)], vs_sem.at[d], vr_sem.at[d], member(0, d))
         for d in range(1, B)
     ]
 
@@ -167,56 +221,82 @@
 
     shared = PODS % 2 == 0
     mate = o + 1 - 2 * (o % 2)
-    if shared:
-        half = pl.ds(pl.multiple_of((o % 2) * (N // 2), N // 2), N // 2)
-    else:
-        half = pl.ds(0, N)
-    w_copies, m_copies = [], []
-    for d in range(1, B):
-        w_copies.append(remote(
-            wq.at[shard_of(b), half], wq.at[shard_of(b), half],
-            ws_sem.at[0, d], wr_sem.at[0, d], member(0, d),
-        ))
-        if shared:
-            came = (b - d + B) % B
-            m_copies.append(remote(
-                wq.at[shard_of(came), half], wq.at[shard_of(came), half],
-                ws_sem.at[1, d], wr_sem.at[1, d], {"outer": mate},
-            ))
-
-    ins[0].wait()
-    for cp in x_copies:
-        cp.start()
-    ins[1].wait()
-    for cp in b_copies:
-        cp.start()
-    ins[2].wait()
-    for cp in w_copies:
-        cp.start()
-    ins[3].wait()
-    for k in range(K):
+    base, WN = (o % 2 * (N // 2), N // 2 // PIECES) if shared else (0, N // PIECES)
+    w_copies, m_copies = [[] for _ in range(PIECES)], [[] for _ in range(PIECES)]
+    for i in range(PIECES):
+        piece = pl.ds(pl.multiple_of(base + i * WN, WN), WN)
+        for d in range(1, B):
+            here = wq.at[shard_of(b), piece]
+            w_copies[i].append(
+                remote(here, here, ws_sem.at[0, i, d], wr_sem.at[0, i, d], member(0, d))
+            )
+            if shared:
+                came = wq.at[shard_of((b - d + B) % B), piece]
+                m_copies[i].append(
+                    remote(came, came, ws_sem.at[1, i, d], wr_sem.at[1, i, d], {"outer": mate})
+                )
+
+    def g_first(k):
         for direction in range(2):
             @pl.when(g_sends(direction, 1))
             def _():
                 g_copy(direction, 1, k).start()
-    ins[4].wait()
-    ins[5].wait()
+
+    ins[0].wait()
+    for cp in c_copies:
+        cp.start()
+    ins[1].wait()
+    for cp in x_copies:
+        cp.start()
+    ins[2].wait()
+    for k in range(AHEAD):
+        g_first(k)
+    ins[3].wait()
+    for cp in w_copies[0]:
+        cp.start()
+    for cp in ins[4:]:
+        cp.wait()
 
     for k in range(K):
         high, low = halves(ev[:, cols[k]])
         eh[:, cols[k]] = high.astype(BF16)
         el[:, cols[k]] = low.astype(BF16)
-    fed = thin_dot(bas[0], eh[...], el[...], 1)
+    fed = thin_dot(bas[...], eh[...], el[...], 1)
+
+    for cp in c_copies:
+        cp.wait_recv()
+    for cp in v_copies + b_copies[0]:
+        cp.start()
+    for copies in w_copies[1:]:
+        for cp in copies:
+            cp.start()
+    ball[0, :, :, share_of(o)] = bz[...]
+    for d in range(1, B):
+        v_copies[B - d - 1].wait_recv()
+        for cp in b_copies[d]:
+            cp.start()
+    for copies in b_copies:
+        for cp in copies:
+            cp.wait_recv()
+    thin = jnp.zeros((B * A * R, T), F32)
+    for k in range(K):
+        basis = split(jnp.concatenate(
+            [ball[d, t, :, cols[k]] for d in range(B) for t in range(A)], axis=0
+        ))
+        thin = thin + fold(dot(basis, gg[rows_of(a), cols[k]], 1, 1))
+    for d in range(B):
+        for t in range(A):
+            row = (d * A + t) * R
+            shard = shard_of(t * B + (b + d) % B)
+            ls[t, d] = fold(dot(split(thin[row : row + R, :]), xv[:, shard], 1, 0)) / TOK_DEV
+    j_copies = along(lambda t: ls.at[t], lz.at[a], js_sem, jr_sem)
+    for cp in j_copies:
+        cp.start()
+    lz[a] = ls[a]
 
     for cp in x_copies:
         cp.wait_recv()
     xt[...] = xg[...].T
-    for cp in b_copies:
-        cp.wait_recv()
-    for cp in w_copies:
-        cp.wait_recv()
-    for cp in m_copies:
-        cp.start()
 
     def y_copy(d, k):
         return remote(
@@ -237,10 +317,6 @@
             y_copy(d, k).wait_recv()
             part = part + yrecv[d - 1, :, cols[k]].astype(F32)
         ne_ref[:, cols[k]] = part / TOK_DEV + ev[:, cols[k]]
-
-    def project_chunk(k):
-        basis = split(jnp.concatenate([bas[d, :, cols[k]] for d in range(B)], axis=0))
-        return fold(dot(basis, gg[:, cols[k]], 1, 1))
 
     def o_copy(direction, r, k):
         s_buf, r_buf = (up_s, up_r) if direction == 0 else (dn_s, dn_r)
@@ -277,21 +353,130 @@
             s_buf[r - 1, :, cols[k]] = part.astype(BF16)
             o_copy(direction, r, k).start()
 
-    def out_pieces(r, ks, first):
-        for k in ks:
-            for direction in range(2):
-                out_piece(direction, r, k, first)
-
-    early, held = range(K - HELD), range(K - HELD, K)
-    l_copies = [
-        remote(left_s, left_r.at[j], ls_sem.at[j], lr_sem.at[j], member(do, db))
-        for j, (do, db) in enumerate(group)
+    def weights_in():
+        for came, passed in zip(w_copies, m_copies):
+            for cp in came:
+                cp.wait_recv()
+            for cp in passed:
+                cp.start()
+
+    def mates_in():
+        for copies in m_copies:
+            for cp in copies:
+                cp.wait_recv()
+
+    def first_piece(r, k):
+        for direction in range(2):
+            out_piece(direction, r, k, True)
+
+    def rest_piece(r, k):
+        for direction in range(2):
+            out_piece(direction, r, k, False)
+
+    l_copies = across(lambda do, db: left_s, lambda j, db: left_r.at[j], ls_sem, lr_sem)
+    z_copies = along(lambda t: zs.at[t], zr.at[a], zs_sem, zr_sem)
+    h_copies = across(
+        lambda do, db: rp.at[db, :, :, share_of((o + do) % PODS)],
+        lambda j, db: rq.at[j], hs_sem, hr_sem,
+    )
+    t_copies = along(lambda t: rs.at[t], rw.at[a], ts_sem, tr_sem)
+    a_copies = along(lambda t: rz.at[a], rz.at[a], as_sem, ar_sem)
+    p_copies = [
+        remote(
+            rz.at[a], rown.at[:, share_of(o)], ps_sem.at[do], pr_sem.at[do], member(do, 0)
+        )
+        for do in range(1, PODS)
     ]
-    thin = jnp.zeros((B * R, A * T), F32)
-    last = A - 2 + K
-    for wave in range(1, last + 1):
+    f_copies = across(
+        lambda do, db: rz, lambda j, db: rall.at[(-db) % B, :, :, share_of(o)], fs_sem, fr_sem
+    )
+
+    def left_line():
+        for cp in j_copies:
+            cp.wait_recv()
+        for d in range(B):
+            part = lz[0, d]
+            for t in range(1, A):
+                part = part + lz[t, d]
+            left_s[d] = part + fed if d == 0 else part
+        for cp in l_copies:
+            cp.start()
+
+    left = []
+
+    def left_done():
+        total = [left_s[d] for d in range(B)]
+        for j, (do, db) in enumerate(group):
+            l_copies[j].wait_recv()
+            for d in range(B):
+                total[d] = total[d] + left_r[j, (d + db) % B]
+        left.extend(orthonormal(total[d] / PODS) for d in range(B))
+        z = jnp.concatenate(
+            [fold(dot(split(left[d]), xt[shard_of((b + d) % B), :], 1, 0)) for d in range(B)],
+            axis=0,
+        )
+        for t in range(A):
+            zs[t] = z[:, t * T : (t + 1) * T]
+        for cp in z_copies:
+            cp.start()
+        zr[a] = zs[a]
+
+    z_all = []
+
+    def right_part():
+        for cp in z_copies:
+            cp.wait_recv()
+        z_all.append(split(jnp.concatenate(
+            [zr[t, d * R : (d + 1) * R, :] for d in range(B) for t in range(A)], axis=0
+        )))
+        for k in range(K):
+            part = fold(dot(z_all[0], gg[rows_of(a), cols[k]], 1, 0)) / TOK_DEV
+            lead = thin_dot(left[0], eh[:, cols[k]], el[:, cols[k]], 0)
+            for d in range(B):
+                for t in range(A):
+                    row = (d * A + t) * R
+                    piece = part[row : row + R]
+                    if d == 0:
+                        piece = piece + jnp.where(a == t, lead, 0.0)
+                    rp[d, t, :, cols[k]] = piece.astype(BF16)
+        for cp in h_copies:
+            cp.start()
+
+    def right_group():
+        right = rp[0, :, :, share_of(o)].astype(F32)
+        for j, cp in enumerate(h_copies):
+            cp.wait_recv()
+            right = right + rq[j].astype(F32)
+        rs[...] = right.astype(BF16)
+        for cp in t_copies:
+            cp.start()
+        rw[a] = rs[a]
+
+    def right_line():
+        for cp in t_copies:
+            cp.wait_recv()
+        right = rw[0].astype(F32)
+        for t in range(1, A):
+            right = right + rw[t].astype(F32)
+        rz[a] = (right / PODS).astype(BF16)
+        for cp in a_copies + p_copies:
+            cp.start()
+        rown[:, share_of(o)] = rz[a]
+
+    def right_all():
+        for cp in a_copies:
+            cp.wait_recv()
+        for cp in f_copies:
+            cp.start()
+        rall[0, :, :, share_of(o)] = rz[...]
+
+    def own_out():
+        for k in range(K):
+            own[:, cols[k]] = dot(xg[rows_of(a), :], wq[:, cols[k]], 1, 0)
+
+    def wave(step):
         for h in range(1, A):
-            k = wave - h
+            k = step - h
             if 0 <= k < K:
                 for direction in range(2):
                     @pl.when(g_gets(direction, h))
@@ -301,102 +486,22 @@
                         @pl.when(g_sends(direction, h + 1))
                         def _():
                             g_copy(direction, h + 1, k).start()
-        if wave == 1:
-            for cp in m_copies:
-                cp.wait_recv()
-            for r in range(A - 1, 1, -1):
-                out_pieces(r, range(K), True)
-            out_pieces(1, early, True)
-            for k in range(K):
-                own[:, cols[k]] = dot(xg[rows_of(a), :], wq[:, cols[k]], 1, 0)
-        k = wave - (A - 1)
+        k = step - 1 + AHEAD
+        if k < K:
+            g_first(k)
+        k = step - (A - 1)
         if 0 <= k < K:
-            thin = thin + project_chunk(k)
-            if k == K - 1:
-                for d in range(B):
-                    mine = thin[d * R : (d + 1) * R, :]
-                    part = fold(dot(split(mine), xg[:, shard_of((b + d) % B)], 1, 0)) / TOK_DEV
-                    left_s[d] = part + fed if d == 0 else part
-                for cp in l_copies:
-                    cp.start()
             gradient_chunk(k)
-            if k >= 1:
-                merge_chunk(k - 1)
-    for r in range(A - 2, 1, -1):
-        out_pieces(r, range(K), False)
-
-    total = [left_s[d] for d in range(B)]
-    for j, (do, db) in enumerate(group):
-        l_copies[j].wait_recv()
-        for d in range(B):
-            total[d] = total[d] + left_r[j, (d + db) % B]
-    left = [orthonormal(total[d] / PODS) for d in range(B)]
-
-    z = jnp.concatenate(
-        [fold(dot(split(left[d]), xt[shard_of((b + d) % B), :], 1, 0)) for d in range(B)], axis=0
-    )
-    for t in range(A):
-        zs[t] = z[:, t * T : (t + 1) * T]
-    z_copies = []
-    for d in range(1, A):
-        t = (a + d) % A
-        z_copies.append(remote(
-            zs.at[t], zr.at[a], zs_sem.at[d], zr_sem.at[d], {"chip": t * B + b}
-        ))
-    z_pair = split(z)
-    for k in range(K):
-        part = fold(dot(z_pair, gg[:, cols[k]], 1, 0)) / TOK_DEV
-        lead = part[:R] + thin_dot(left[0], eh[:, cols[k]], el[:, cols[k]], 0)
-        rp[0, :, cols[k]] = lead.astype(BF16)
-        for d in range(1, B):
-            rp[d, :, cols[k]] = part[d * R : (d + 1) * R].astype(BF16)
-    h_copies = [
-        remote(
-            rp.at[db, :, share_of((o + do) % PODS)], rq.at[j],
-            hs_sem.at[j], hr_sem.at[j], member(do, db),
-        )
-        for j, (do, db) in enumerate(group)
-    ]
-    for cp in h_copies:
-        cp.start()
-    for cp in z_copies:
-        cp.start()
-    zr[a] = zs[a]
-    out_pieces(1, early, False)
-
-    right = rp[0, :, share_of(o)].astype(F32)
-    for j, cp in enumerate(h_copies):
-        cp.wait_recv()
-        right = right + rq[j].astype(F32)
-    rz[a] = (right / PODS).astype(BF16)
-    p_copies = [
-        remote(
-            rz.at[a], rown.at[:, share_of(o)], ps_sem.at[do], pr_sem.at[do], member(do, 0)
-        )
-        for do in range(1, PODS)
-    ]
-    a_copies = [
-        remote(rz.at[a], rz.at[a], as_sem.at[d + 1], ar_sem.at[d + 1], {"chip": t})
-        for d, t in enumerate(line)
-    ]
-    for cp in a_copies + p_copies:
-        cp.start()
-    rown[:, share_of(o)] = rz[a]
-    for first in (True, False):
-        out_pieces(1, held, first)
-    merge_chunk(K - 1)
-
-    for cp in a_copies:
-        cp.wait_recv()
-    f_copies = [
-        remote(
-            rz, rall.at[(-db) % B, :, :, share_of(o)], fs_sem.at[j], fr_sem.at[j], member(do, db)
-        )
-        for j, (do, db) in enumerate(group)
-    ]
-    for cp in f_copies:
-        cp.start()
-    rall[0, :, :, share_of(o)] = rz[...]
+
+    actions = {
+        "wave": wave, "weights": weights_in, "mates": mates_in, "left1": left_line,
+        "left2": left_done, "right1": right_part, "right2": right_group,
+        "right3": right_line, "right4": right_all, "own": own_out,
+        "first": first_piece, "rest": rest_piece, "merge": merge_chunk,
+    }
+    for kind, *args in plan_of(A, K):
+        actions[kind](*args)
+
     for cp in p_copies:
         cp.wait_recv()
     lefts = split(left[0])
@@ -404,18 +509,13 @@
         mine = rown[:, cols[k]].astype(F32)
         ne_ref[:, cols[k]] = ne_ref[:, cols[k]] - dot(lefts, stack(mine, mine), 0, 0)
 
-    for cp in z_copies:
-        cp.wait_recv()
-    z = split(jnp.concatenate(
-        [zr[t, d * R : (d + 1) * R, :] for d in range(B) for t in range(A)], axis=0
-    ))
     for cp in f_copies:
         cp.wait_recv()
     for k in range(K):
         rights = jnp.concatenate(
             [rall[d, t, :, cols[k]].astype(F32) for d in range(B) for t in range(A)], axis=0
         )
-        delta = dot(z, stack(rights, rights), 0, 0)
+        delta = dot(z_all[0], stack(rights, rights), 0, 0)
         for direction in range(2):
             r_buf = up_r if direction == 0 else dn_r
 
@@ -429,9 +529,12 @@
         mine = own[:, cols[k]] + up_r[0, :, cols[k]].astype(F32) + dn_r[0, :, cols[k]].astype(F32)
         out_ref[:, cols[k]] = (mine - LEARNING_RATE * delta).astype(BF16)
 
-    for cp in x_copies + b_copies + w_copies + m_copies + l_copies + z_copies + h_copies:
+    for copies in b_copies + w_copies + m_copies:
+        for cp in copies:
+            cp.wait_send()
+    for cp in c_copies + v_copies + x_copies + j_copies + l_copies:
         cp.wait_send()
-    for cp in p_copies + a_copies + f_copies:
+    for cp in z_copies + h_copies + t_copies + p_copies + a_copies + f_copies:
         cp.wait_send()
     for k in range(K):
         for d in range(1, B):
@@ -475,7 +578,9 @@
             pltpu.VMEM((Q, A * T), BF16),
             pltpu.VMEM((A * T, N), BF16),
             pltpu.VMEM((Q, N), BF16),
-            pltpu.VMEM((B, R, N), F32),
+            pltpu.VMEM((R, N), F32),
+            pltpu.VMEM((A, R, N // PODS), F32),
+            pltpu.VMEM((B, A, R, N), F32),
             pltpu.VMEM((S, N), F32),
             pltpu.VMEM((S, N), BF16),
             pltpu.VMEM((S, N), BF16),
@@ -485,27 +590,36 @@
             pltpu.VMEM((A - 1, T, N), BF16),
             pltpu.VMEM((A - 1, T, N), BF16),
             pltpu.VMEM((A - 1, T, N), BF16),
+            pltpu.VMEM((A, B, R, S), F32),
+            pltpu.VMEM((A, B, R, S), F32),
             pltpu.VMEM((B, R, S), F32),
             pltpu.VMEM((G - 1, B, R, S), F32),
             pltpu.VMEM((A, B * R, T), F32),
             pltpu.VMEM((A, B * R, T), F32),
-            pltpu.VMEM((B, R, N), BF16),
-            pltpu.VMEM((G - 1, R, N // PODS), BF16),
+            pltpu.VMEM((B, A, R, N), BF16),
+            pltpu.VMEM((G - 1, A, R, N // PODS), BF16),
+            pltpu.VMEM((A, R, N // PODS), BF16),
+            pltpu.VMEM((A, R, N // PODS), BF16),
             pltpu.VMEM((A, R, N // PODS), BF16),
             pltpu.VMEM((R, N), BF16),
             pltpu.VMEM((B, A, R, N), BF16),
             pltpu.VMEM((T, N), F32),
-            dma((6,)), dma((A,)), dma((A,)), dma((2, B)), dma((2, B)), dma((B,)), dma((B,)),
-            dma((2, A, K)), dma((2, A, K)), dma((B, K)), dma((B, K)),
+            dma((7,)), dma((A,)), dma((A,)), dma((2, PIECES, B)), dma((2, PIECES, B)),
+            dma((A,)), dma((A,)), dma((B,)), dma((B,)), dma((B, PODS)), dma((B, PODS)),
             dma((2, A, K)), dma((2, A, K)),
-            dma((G,)), dma((G,)), dma((A,)), dma((A,)), dma((G,)), dma((G,)),
+            dma((B, K)), dma((B, K)), dma((2, A, K)), dma((2, A, K)),
+            dma((A,)), dma((A,)), dma((G,)), dma((G,)), dma((A,)), dma((A,)),
+            dma((G,)), dma((G,)), dma((A,)), dma((A,)),
             dma((PODS,)), dma((PODS,)), dma((A,)), dma((A,)), dma((G,)), dma((G,)),
         ],
         compiler_params=pltpu.CompilerParams(
             collective_id=0, has_side_effects=True, vmem_limit_bytes=40 * 1024 * 1024
         ),
         name="step",
-    )(inputs, out_grads, weight, start_basis, error_buffer[0])
+    )(*[
+        pltpu.with_memory_space_constraint(t, pltpu.HBM)
+        for t in (inputs, out_grads, weight, start_basis, error_buffer[0])
+    ])
     return outputs, new_error[None]
 
 

time: 91.4 us -> 78.3 us (0.86)
  Pallas kernels: 82.6 us -> 75.4 us
  local copies, waits for them, and re-layouts: 7.84 us -> 2.11 us
    pallas_call x1, Pallas kernels: 82.6 us -> 75.4 us  [shards(): pl.pallas_call(functools.partial(kernel, A, B, PODS), out_shape=(jax.Shap...]
    unnamed x12 -> x2, local copies, waits for them, and re-layouts: 7.84 us -> 2.11 us
where the time goes in v2:
time: 78.3 us; the launch traced here: 78.1 us
  Pallas kernels  75.4 us (96%)
  local copies, waits for them, and re-layouts  2.11 us (3%)
    pallas_call x1, Pallas kernels, shards(): pl.pallas_call(functools.partial(kernel, A, B, PODS), out_shape=(jax.Shap...  75.4 us
    unnamed x2, local copies, waits for them, and re-layouts  2.11 us

profile of v2, /device:TPU:0, one launch (start us, length us, event | category | flops | bytes accessed | tf_op | source)
XLA Modules:
  0.0 78.1 jit_solution(17898486942617048851)
XLA Ops:
  0.6 75.4 %step.1 = (bf16[128,2048]{1,0:T(8,128)(2,1)S(1)}, f32[256,2048]{1,0:T(8,128)S(1)}) custom-call(bf16[128,2048]{1,0:T(8,128)(2,1)} %x_hbm.1, bf16[128,2048]{1,0:T(8,128)(2,1)} %g_hbm.1, bf16[256,2048]{1,0:T(8,128)(2,1)} %w_hbm.1, f32[8,2048]{1,0:T(8,128)} %basis_hbm.1, f32[256,2048]{1,0:T(8,128)} %bitcast.3), custom_call_target="tpu_custom_call" | custom-call | tf_op jit(solution)/shard_map/step/pallas_call | solution.py:567
  76.0 0.8 %copy.9 = bf16[128,2048]{1,0:T(8,128)(2,1)} copy(bf16[128,2048]{1,0:T(8,128)(2,1)S(1)} %get-tuple-element.8) | data formatting | bytes 1048576
  76.8 1.3 %copy.10 = f32[1,256,2048]{2,1,0:T(8,128)} copy(f32[1,256,2048]{2,1,0:T(8,128)S(1)} %bitcast.2) | data formatting | bytes 4194304

commit v3 on v2

--- a/solution.py
+++ b/solution.py
@@ -12,6 +12,7 @@
 CHUNKS = 8
 AHEAD = 4
 PIECES = 2
+FAMILIES = "abcfhjlmptvxyzw"
 F32 = jnp.float32
 BF16 = jnp.bfloat16
 
@@ -70,7 +71,7 @@
 
     last = A - 2 + K
     chain = {
-        2: ["weights", "mates"], 3: ["left1"], 5: ["left2", "own"], last - 3: ["right1"],
+        1: ["basis"], 2: ["left0", "x", "weights", "mates"], 3: ["left1"], 5: ["left2", "own"], last - 3: ["right1"],
         last - 2: ["right2"], last - 1: ["right3"],
     }
     steps = []
@@ -93,9 +94,7 @@
     out_ref, ne_ref,
     xv, xg, xt, gg, wq, bas, bz, ball, ev, eh, el, ysend, yrecv, up_s, up_r, dn_s, dn_r,
     ls, lz, left_s, left_r, zs, zr, rp, rq, rs, rw, rz, rown, rall, own,
-    in_sem, xs_sem, xr_sem, ws_sem, wr_sem, cs_sem, cr_sem, vs_sem, vr_sem, bs_sem, br_sem,
-    gs_sem, gr_sem, ys_sem, yr_sem, rs_sem, rr_sem, js_sem, jr_sem, ls_sem, lr_sem, zs_sem, zr_sem,
-    hs_sem, hr_sem, ts_sem, tr_sem, ps_sem, pr_sem, as_sem, ar_sem, fs_sem, fr_sem,
+    in_sem, send_sem, recv_sem, gs_sem, gr_sem, yr_sem, rs_sem, rr_sem,
 ):
     o = lax.axis_index("outer")
     c = lax.axis_index("chip")
@@ -156,39 +155,62 @@
         )
     pl.semaphore_wait(barrier, len(line) + len(group))
 
-    x_copies = []
-    for d in range(1, A):
-        t = (a + d) % A
-        x_copies.append(remote(
-            xv.at[:, pl.ds(pl.multiple_of(t * Q, Q), Q)], xg.at[rows_of(a)],
-            xs_sem.at[d], xr_sem.at[d], {"chip": t * B + b},
-        ))
-    def along(src, dst, ss, rs):
+    def family(name, step=0):
+        i = FAMILIES.index(name)
+        return send_sem.at[i], recv_sem.at[i + step]
+
+    def along(src, dst, name):
         return [
-            remote(src((a + d) % A), dst, ss.at[d], rs.at[d], {"chip": ((a + d) % A) * B + b})
+            remote(src((a + d) % A), dst, *family(name), {"chip": ((a + d) % A) * B + b})
             for d in range(1, A)
         ]
 
-    def across(src, dst, ss, rs):
+    def across(src, dst, name):
         return [
-            remote(src(do, db), dst(j, db), ss.at[j], rs.at[j], member(do, db))
+            remote(src(do, db), dst(j, db), *family(name), member(do, db))
             for j, (do, db) in enumerate(group)
         ]
 
-    c_copies = along(lambda t: bz.at[a], bz.at[a], cs_sem, cr_sem)
+    def whole(ref, name, step=0):
+        return remote(ref, ref, *family(name, step), {"outer": (o + 1) % PODS})
+
+    def start(copies):
+        for cp in copies:
+            cp.start()
+
+    lines = pl.ds(0, A - 1)
+    others = pl.ds(0, (PODS - 1) * NP)
+    x_all = whole(xg.at[pl.ds(0, (A - 1) * T)], "x")
+    c_all = whole(bz.at[lines], "c")
+    v_all = whole(ball.at[pl.ds(0, B - 1), :, :, pl.ds(0, NP)], "v")
+    b_all = whole(ball.at[:, :, :, others], "b")
+    j_all = whole(ls.at[lines], "j")
+    l_all = whole(left_r, "l")
+    z_all = whole(zs.at[lines], "z")
+    h_all = whole(rq, "h")
+    t_all = whole(rs.at[lines], "t")
+    p_all = whole(rown.at[:, others], "p")
+    a_all = whole(rz.at[lines], "a")
+    f_all = whole(rq, "f")
+    y_all = whole(ysend, "y")
+
+    x_copies = along(
+        lambda t: xv.at[:, pl.ds(pl.multiple_of(t * Q, Q), Q)], xg.at[rows_of(a)], "x"
+    )
+    c_copies = along(lambda t: bz.at[a], bz.at[a], "c")
     b_copies = [
         [
             remote(
                 bz if d == 0 else ball.at[d, :, :, share_of(o)],
                 ball.at[d, :, :, share_of(o)],
-                bs_sem.at[d, do], br_sem.at[d, do], member(do, 0),
+                *family("b"), member(do, 0),
             )
             for do in range(1, PODS)
         ]
         for d in range(B)
     ]
     v_copies = [
-        remote(bz, ball.at[(-d) % B, :, :, share_of(o)], vs_sem.at[d], vr_sem.at[d], member(0, d))
+        remote(bz, ball.at[(-d) % B, :, :, share_of(o)], *family("v"), member(0, d))
         for d in range(1, B)
     ]
 
@@ -197,7 +219,7 @@
         source = a - step * (h - 1)
         place = gg.at[rows_of(source), cols[k]]
         return remote(
-            place, place, gs_sem.at[direction, h, k], gr_sem.at[direction, h, k],
+            place, place, gs_sem.at[direction, h - 1], gr_sem.at[source, k],
             {"chip": c + step * B},
         )
 
@@ -213,9 +235,10 @@
 
     def g_arrival(direction, h, k):
         step = 1 if direction == 0 else -1
-        place = gg.at[rows_of(a - step * h), cols[k]]
+        source = a - step * h
+        place = gg.at[rows_of(source), cols[k]]
         return remote(
-            place, place, gs_sem.at[direction, h, k], gr_sem.at[direction, h, k],
+            place, place, gs_sem.at[direction, h - 1], gr_sem.at[source, k],
             {"chip": c - step * B},
         )
 
@@ -227,14 +250,14 @@
         piece = pl.ds(pl.multiple_of(base + i * WN, WN), WN)
         for d in range(1, B):
             here = wq.at[shard_of(b), piece]
-            w_copies[i].append(
-                remote(here, here, ws_sem.at[0, i, d], wr_sem.at[0, i, d], member(0, d))
-            )
+            w_copies[i].append(remote(here, here, *family("w", i), member(0, d)))
             if shared:
                 came = wq.at[shard_of((b - d + B) % B), piece]
-                m_copies[i].append(
-                    remote(came, came, ws_sem.at[1, i, d], wr_sem.at[1, i, d], {"outer": mate})
-                )
+                m_copies[i].append(remote(came, came, *family("m"), {"outer": mate}))
+    rest = pl.ds(0, (B - 1) * S)
+    w_part = [whole(wq.at[rest, pl.ds(0, WN)], "w", i) for i in range(PIECES)]
+    w_all = whole(wq.at[rest, pl.ds(0, PIECES * WN)], "w")
+    m_all = whole(wq.at[rest, pl.ds(0, PIECES * WN)], "m")
 
     def g_first(k):
         for direction in range(2):
@@ -243,17 +266,14 @@
                 g_copy(direction, 1, k).start()
 
     ins[0].wait()
-    for cp in c_copies:
-        cp.start()
+    start(c_copies)
     ins[1].wait()
-    for cp in x_copies:
-        cp.start()
+    start(x_copies)
     ins[2].wait()
     for k in range(AHEAD):
         g_first(k)
     ins[3].wait()
-    for cp in w_copies[0]:
-        cp.start()
+    start(w_copies[0])
     for cp in ins[4:]:
         cp.wait()
 
@@ -263,45 +283,15 @@
         el[:, cols[k]] = low.astype(BF16)
     fed = thin_dot(bas[...], eh[...], el[...], 1)
 
-    for cp in c_copies:
-        cp.wait_recv()
-    for cp in v_copies + b_copies[0]:
-        cp.start()
+    c_all.wait_recv()
+    start(v_copies + b_copies[0])
     for copies in w_copies[1:]:
-        for cp in copies:
-            cp.start()
+        start(copies)
     ball[0, :, :, share_of(o)] = bz[...]
-    for d in range(1, B):
-        v_copies[B - d - 1].wait_recv()
-        for cp in b_copies[d]:
-            cp.start()
-    for copies in b_copies:
-        for cp in copies:
-            cp.wait_recv()
-    thin = jnp.zeros((B * A * R, T), F32)
-    for k in range(K):
-        basis = split(jnp.concatenate(
-            [ball[d, t, :, cols[k]] for d in range(B) for t in range(A)], axis=0
-        ))
-        thin = thin + fold(dot(basis, gg[rows_of(a), cols[k]], 1, 1))
-    for d in range(B):
-        for t in range(A):
-            row = (d * A + t) * R
-            shard = shard_of(t * B + (b + d) % B)
-            ls[t, d] = fold(dot(split(thin[row : row + R, :]), xv[:, shard], 1, 0)) / TOK_DEV
-    j_copies = along(lambda t: ls.at[t], lz.at[a], js_sem, jr_sem)
-    for cp in j_copies:
-        cp.start()
-    lz[a] = ls[a]
-
-    for cp in x_copies:
-        cp.wait_recv()
-    xt[...] = xg[...].T
-
     def y_copy(d, k):
         return remote(
             ysend.at[d - 1, :, cols[k]], yrecv.at[d - 1, :, cols[k]],
-            ys_sem.at[d, k], yr_sem.at[d, k], member(0, d),
+            family("y")[0], yr_sem.at[d - 1, k], member(0, d),
         )
 
     def gradient_chunk(k):
@@ -322,8 +312,17 @@
         s_buf, r_buf = (up_s, up_r) if direction == 0 else (dn_s, dn_r)
         return remote(
             s_buf.at[r - 1, :, cols[k]], r_buf.at[r - 1, :, cols[k]],
-            rs_sem.at[direction, r, k], rr_sem.at[direction, r, k],
+            rs_sem.at[direction, r - 1], rr_sem.at[a + r + 1 if direction == 0 else a - r, k],
             {"chip": c + B if direction == 0 else c - B},
+        )
+
+    def o_arrival(direction, r, k):
+        r_buf = up_r if direction == 0 else dn_r
+        place = r_buf.at[r - 1, :, cols[k]]
+        return remote(
+            place, place, rs_sem.at[direction, r - 1],
+            rr_sem.at[a + r if direction == 0 else a + 1 - r, k],
+            {"chip": c - B if direction == 0 else c + B},
         )
 
     def o_first(direction):
@@ -348,22 +347,45 @@
             token = a + r if direction == 0 else a - r
             part = dot(xg[rows_of(token), :], wq[:, cols[k]], 1, 0)
             if not first:
-                o_copy(direction, r + 1, k).wait_recv()
+                o_arrival(direction, r + 1, k).wait_recv()
                 part = part + r_buf[r, :, cols[k]].astype(F32)
             s_buf[r - 1, :, cols[k]] = part.astype(BF16)
             o_copy(direction, r, k).start()
 
+    def basis_pass():
+        v_all.wait_recv()
+        for d in range(1, B):
+            start(b_copies[d])
+
+    def left_part():
+        b_all.wait_recv()
+        thin = jnp.zeros((B * A * R, T), F32)
+        for k in range(K):
+            basis = split(jnp.concatenate(
+                [ball[d, t, :, cols[k]] for d in range(B) for t in range(A)], axis=0
+            ))
+            thin = thin + fold(dot(basis, gg[rows_of(a), cols[k]], 1, 1))
+        for d in range(B):
+            for t in range(A):
+                row = (d * A + t) * R
+                shard = shard_of(t * B + (b + d) % B)
+                ls[t, d] = fold(dot(split(thin[row : row + R, :]), xv[:, shard], 1, 0)) / TOK_DEV
+        start(j_copies)
+        lz[a] = ls[a]
+
+
+    def x_in():
+        x_all.wait_recv()
+        xt[...] = xg[...].T
+
     def weights_in():
-        for came, passed in zip(w_copies, m_copies):
-            for cp in came:
-                cp.wait_recv()
-            for cp in passed:
-                cp.start()
+        for came, passed in zip(w_part, m_copies):
+            came.wait_recv()
+            start(passed)
 
     def mates_in():
-        for copies in m_copies:
-            for cp in copies:
-                cp.wait_recv()
+        if shared:
+            m_all.wait_recv()
 
     def first_piece(r, k):
         for direction in range(2):
@@ -373,41 +395,38 @@
         for direction in range(2):
             out_piece(direction, r, k, False)
 
-    l_copies = across(lambda do, db: left_s, lambda j, db: left_r.at[j], ls_sem, lr_sem)
-    z_copies = along(lambda t: zs.at[t], zr.at[a], zs_sem, zr_sem)
+    j_copies = along(lambda t: ls.at[t], lz.at[a], "j")
+    l_copies = across(lambda do, db: left_s, lambda j, db: left_r.at[j], "l")
+    z_copies = along(lambda t: zs.at[t], zr.at[a], "z")
     h_copies = across(
         lambda do, db: rp.at[db, :, :, share_of((o + do) % PODS)],
-        lambda j, db: rq.at[j], hs_sem, hr_sem,
+        lambda j, db: rq.at[j], "h",
     )
-    t_copies = along(lambda t: rs.at[t], rw.at[a], ts_sem, tr_sem)
-    a_copies = along(lambda t: rz.at[a], rz.at[a], as_sem, ar_sem)
+    t_copies = along(lambda t: rs.at[t], rw.at[a], "t")
+    a_copies = along(lambda t: rz.at[a], rz.at[a], "a")
     p_copies = [
-        remote(
-            rz.at[a], rown.at[:, share_of(o)], ps_sem.at[do], pr_sem.at[do], member(do, 0)
-        )
+        remote(rz.at[a], rown.at[:, share_of(o)], *family("p"), member(do, 0))
         for do in range(1, PODS)
     ]
     f_copies = across(
-        lambda do, db: rz, lambda j, db: rall.at[(-db) % B, :, :, share_of(o)], fs_sem, fr_sem
+        lambda do, db: rz, lambda j, db: rall.at[(-db) % B, :, :, share_of(o)], "f"
     )
 
     def left_line():
-        for cp in j_copies:
-            cp.wait_recv()
+        j_all.wait_recv()
         for d in range(B):
             part = lz[0, d]
             for t in range(1, A):
                 part = part + lz[t, d]
             left_s[d] = part + fed if d == 0 else part
-        for cp in l_copies:
-            cp.start()
+        start(l_copies)
 
     left = []
 
     def left_done():
         total = [left_s[d] for d in range(B)]
+        l_all.wait_recv()
         for j, (do, db) in enumerate(group):
-            l_copies[j].wait_recv()
             for d in range(B):
                 total[d] = total[d] + left_r[j, (d + db) % B]
         left.extend(orthonormal(total[d] / PODS) for d in range(B))
@@ -417,20 +436,18 @@
         )
         for t in range(A):
             zs[t] = z[:, t * T : (t + 1) * T]
-        for cp in z_copies:
-            cp.start()
+        start(z_copies)
         zr[a] = zs[a]
 
-    z_all = []
+    z_wide = []
 
     def right_part():
-        for cp in z_copies:
-            cp.wait_recv()
-        z_all.append(split(jnp.concatenate(
+        z_all.wait_recv()
+        z_wide.append(split(jnp.concatenate(
             [zr[t, d * R : (d + 1) * R, :] for d in range(B) for t in range(A)], axis=0
         )))
         for k in range(K):
-            part = fold(dot(z_all[0], gg[rows_of(a), cols[k]], 1, 0)) / TOK_DEV
+            part = fold(dot(z_wide[0], gg[rows_of(a), cols[k]], 1, 0)) / TOK_DEV
             lead = thin_dot(left[0], eh[:, cols[k]], el[:, cols[k]], 0)
             for d in range(B):
                 for t in range(A):
@@ -439,35 +456,29 @@
                     if d == 0:
                         piece = piece + jnp.where(a == t, lead, 0.0)
                     rp[d, t, :, cols[k]] = piece.astype(BF16)
-        for cp in h_copies:
-            cp.start()
+        start(h_copies)
 
     def right_group():
         right = rp[0, :, :, share_of(o)].astype(F32)
-        for j, cp in enumerate(h_copies):
-            cp.wait_recv()
+        h_all.wait_recv()
+        for j in range(len(group)):
             right = right + rq[j].astype(F32)
         rs[...] = right.astype(BF16)
-        for cp in t_copies:
-            cp.start()
+        start(t_copies)
         rw[a] = rs[a]
 
     def right_line():
-        for cp in t_copies:
-            cp.wait_recv()
+        t_all.wait_recv()
         right = rw[0].astype(F32)
         for t in range(1, A):
             right = right + rw[t].astype(F32)
         rz[a] = (right / PODS).astype(BF16)
-        for cp in a_copies + p_copies:
-            cp.start()
+        start(a_copies + p_copies)
         rown[:, share_of(o)] = rz[a]
 
     def right_all():
-        for cp in a_copies:
-            cp.wait_recv()
-        for cp in f_copies:
-            cp.start()
+        a_all.wait_recv()
+        start(f_copies)
         rall[0, :, :, share_of(o)] = rz[...]
 
     def own_out():
@@ -494,7 +505,7 @@
             gradient_chunk(k)
 
     actions = {
-        "wave": wave, "weights": weights_in, "mates": mates_in, "left1": left_line,
+        "basis": basis_pass, "left0": left_part, "x": x_in, "wave": wave, "weights": weights_in, "mates": mates_in, "left1": left_line,
         "left2": left_done, "right1": right_part, "right2": right_group,
         "right3": right_line, "right4": right_all, "own": own_out,
         "first": first_piece, "rest": rest_piece, "merge": merge_chunk,
@@ -502,26 +513,24 @@
     for kind, *args in plan_of(A, K):
         actions[kind](*args)
 
-    for cp in p_copies:
-        cp.wait_recv()
+    p_all.wait_recv()
     lefts = split(left[0])
     for k in range(K):
         mine = rown[:, cols[k]].astype(F32)
         ne_ref[:, cols[k]] = ne_ref[:, cols[k]] - dot(lefts, stack(mine, mine), 0, 0)
 
-    for cp in f_copies:
-        cp.wait_recv()
+    f_all.wait_recv()
     for k in range(K):
         rights = jnp.concatenate(
             [rall[d, t, :, cols[k]].astype(F32) for d in range(B) for t in range(A)], axis=0
         )
-        delta = dot(z_all[0], stack(rights, rights), 0, 0)
+        delta = dot(z_wide[0], stack(rights, rights), 0, 0)
         for direction in range(2):
             r_buf = up_r if direction == 0 else dn_r
 
             @pl.when(o_gets(direction, 1))
             def _():
-                o_copy(direction, 1, k).wait_recv()
+                o_arrival(direction, 1, k).wait_recv()
 
             @pl.when(jnp.logical_not(o_gets(direction, 1)))
             def _():
@@ -529,25 +538,32 @@
         mine = own[:, cols[k]] + up_r[0, :, cols[k]].astype(F32) + dn_r[0, :, cols[k]].astype(F32)
         out_ref[:, cols[k]] = (mine - LEARNING_RATE * delta).astype(BF16)
 
-    for copies in b_copies + w_copies + m_copies:
-        for cp in copies:
-            cp.wait_send()
-    for cp in c_copies + v_copies + x_copies + j_copies + l_copies:
+    for cp in (
+        x_all, c_all, v_all, b_all, w_all, j_all, l_all, z_all, h_all, t_all, p_all, a_all, f_all,
+        y_all,
+    ):
         cp.wait_send()
-    for cp in z_copies + h_copies + t_copies + p_copies + a_copies + f_copies:
-        cp.wait_send()
-    for k in range(K):
-        for d in range(1, B):
-            y_copy(d, k).wait_send()
-        for direction in range(2):
-            for h in range(1, A):
-                @pl.when(g_sends(direction, h))
-                def _():
-                    g_copy(direction, h, k).wait_send()
-
-                @pl.when(o_sends(direction, h))
-                def _():
-                    o_copy(direction, h, k).wait_send()
+    if shared:
+        m_all.wait_send()
+    for direction in range(2):
+        for h in range(1, A):
+            step = 1 if direction == 0 else -1
+
+            @pl.when(g_sends(direction, h))
+            def _():
+                place = gg.at[rows_of(a - step * (h - 1))]
+                remote(
+                    place, place, gs_sem.at[direction, h - 1], gr_sem.at[0, 0],
+                    {"chip": c + step * B},
+                ).wait_send()
+
+            @pl.when(o_sends(direction, h))
+            def _():
+                place = (up_s if direction == 0 else dn_s).at[h - 1]
+                remote(
+                    place, place, rs_sem.at[direction, h - 1], rr_sem.at[0, 0],
+                    {"chip": c + step * B},
+                ).wait_send()
 
 
 def shards(inputs, out_grads, weight, start_basis, error_buffer):
@@ -567,8 +583,8 @@
     outputs, new_error = pl.pallas_call(
         functools.partial(kernel, A, B, PODS),
         out_shape=(
-            jax.ShapeDtypeStruct((T, N), BF16),
-            jax.ShapeDtypeStruct((S, N), F32),
+            pltpu.VMEM((T, N), BF16),
+            pltpu.VMEM((S, N), F32),
         ),
         in_specs=[hbm] * 5,
         out_specs=(vmem, vmem),
@@ -604,13 +620,8 @@
             pltpu.VMEM((R, N), BF16),
             pltpu.VMEM((B, A, R, N), BF16),
             pltpu.VMEM((T, N), F32),
-            dma((7,)), dma((A,)), dma((A,)), dma((2, PIECES, B)), dma((2, PIECES, B)),
-            dma((A,)), dma((A,)), dma((B,)), dma((B,)), dma((B, PODS)), dma((B, PODS)),
-            dma((2, A, K)), dma((2, A, K)),
-            dma((B, K)), dma((B, K)), dma((2, A, K)), dma((2, A, K)),
-            dma((A,)), dma((A,)), dma((G,)), dma((G,)), dma((A,)), dma((A,)),
-            dma((G,)), dma((G,)), dma((A,)), dma((A,)),
-            dma((PODS,)), dma((PODS,)), dma((A,)), dma((A,)), dma((G,)), dma((G,)),
+            dma((7,)), dma((len(FAMILIES),)), dma((len(FAMILIES) + PIECES - 1,)),
+            dma((2, A - 1)), dma((A, K)), dma((B - 1, K)), dma((2, A - 1)), dma((A + 1, K)),
         ],
         compiler_params=pltpu.CompilerParams(
             collective_id=0, has_side_effects=True, vmem_limit_bytes=40 * 1024 * 1024

time: 78.3 us -> 74.3 us (0.949)
  Pallas kernels: 75.4 us -> 71.4 us
    pallas_call x1, Pallas kernels: 75.4 us -> 71.4 us  [shards(): pl.pallas_call(functools.partial(kernel, A, B, PODS), out_shape=(pltpu.VM...]
where the time goes in v3:
time: 74.3 us; the launch traced here: 74.1 us
  Pallas kernels  71.4 us (96%)
  local copies, waits for them, and re-layouts  2.11 us (3%)
    pallas_call x1, Pallas kernels, shards(): pl.pallas_call(functools.partial(kernel, A, B, PODS), out_shape=(pltpu.VM...  71.4 us
    unnamed x2, local copies, waits for them, and re-layouts  2.11 us

profile of v3, /device:TPU:0, one launch (start us, length us, event | category | flops | bytes accessed | tf_op | source)
XLA Modules:
  0.0 74.1 jit_solution(15113079565268226302)
XLA Ops:
  0.6 71.4 %step.1 = (bf16[128,2048]{1,0:T(8,128)(2,1)S(1)}, f32[256,2048]{1,0:T(8,128)S(1)}) custom-call(bf16[128,2048]{1,0:T(8,128)(2,1)} %x_hbm.1, bf16[128,2048]{1,0:T(8,128)(2,1)} %g_hbm.1, bf16[256,2048]{1,0:T(8,128)(2,1)} %w_hbm.1, f32[8,2048]{1,0:T(8,128)} %basis_hbm.1, f32[256,2048]{1,0:T(8,128)} %bitcast.3), custom_call_target="tpu_custom_call" | custom-call | tf_op jit(solution)/shard_map/step/pallas_call | solution.py:583
  72.0 0.8 %copy.9 = bf16[128,2048]{1,0:T(8,128)(2,1)} copy(bf16[128,2048]{1,0:T(8,128)(2,1)S(1)} %get-tuple-element.6) | data formatting | bytes 1048576
  72.8 1.3 %copy.10 = f32[1,256,2048]{2,1,0:T(8,128)} copy(f32[1,256,2048]{2,1,0:T(8,128)S(1)} %bitcast.2) | data formatting | bytes 4194304

commit v4 on v3

--- a/solution.py
+++ b/solution.py
@@ -60,32 +60,58 @@
     return v
 
 
+PLAN = (
+    ("basis",), ("send", 1), ("hop", 1, 1), ("left0",), ("x",), ("hop", 1, 1), ("send", 1),
+    ("hop", 1, 1), ("send", 1), ("hop", 2, 1), ("weights",), ("hop", 1, 1), ("send",),
+    ("hop", 2, 1), ("mates",), ("first", 3), ("grad",), ("hop", 1, 1), ("left1",), ("first", 3),
+    ("hop", 2, 1), ("grad",), ("hop", 1, 1), ("left2",), ("own",), ("hop", 2, 1), ("hop", 1, 1),
+    ("first", 4), ("grad",), ("hop", 1, 1), ("hop", 2, 1), ("rest", 2), ("right1",), ("first", 2),
+    ("grad",), ("hop", 2, 1), ("rest", 3), ("first", 1), ("grad",), ("right2",), ("hop", 2, 1),
+    ("rest", 3), ("first", 4), ("grad",), ("hop", 2, 1), ("outer", 2), ("first", 1), ("right3",),
+    ("grad",), ("rest", 3), ("first", 3), ("outer", 3), ("grad",), ("rest", 2), ("right4",),
+    ("first",), ("outer",), ("rest",), ("y",), ("merge",),
+)
+
+
 def plan_of(A, K):
+    send = [("send", k) for k in range(AHEAD, K)]
+    hops = [[("hop", h, k) for k in range(K)] for h in range(1, A)]
+    grads = list(range(K))
     firsts = [("first", r, k) for r in range(A - 1, 0, -1) for k in range(K)]
-    rests = [("rest", r, k) for r in range(A - 2, 0, -1) for k in range(K)]
+    rests = [("rest", r, k) for r in range(A - 2, 1, -1) for k in range(K)]
+    rests += [("inner", k) for k in range(K)]
+    outers = [("outer", k) for k in range(K)]
+    merges = [("merge", k) for k in range(K)]
+    queues = {"send": send, "first": firsts, "rest": rests, "outer": outers, "merge": merges}
+    steps = []
 
     def take(queue, count):
-        taken = queue[:count]
+        steps.extend(queue[:count])
         del queue[:count]
-        return taken
-
-    last = A - 2 + K
-    chain = {
-        1: ["basis"], 2: ["left0", "x", "weights", "mates"], 3: ["left1"], 5: ["left2", "own"], last - 3: ["right1"],
-        last - 2: ["right2"], last - 1: ["right3"],
-    }
-    steps = []
-    for wave in range(1, last + 1):
-        steps.append(("wave", wave))
-        if wave == last - 2:
-            steps += take(rests, 3)
-        steps += [(name,) for name in chain.get(wave, [])]
-        if wave >= 3:
-            steps += take(firsts, A - 1)
-        if wave >= last - 3:
-            steps += take(rests, 3)
-    steps += [("right4",)] + firsts + rests
-    return steps + [("merge", k) for k in range(K)]
+
+    def gradient():
+        k = grads.pop(0)
+        for h in range(1, A):
+            take(hops[h - 1], K - len(hops[h - 1]) <= k and k + 1 - (K - len(hops[h - 1])))
+        steps.append(("grad", k))
+
+    for kind, *args in PLAN:
+        if kind == "hop":
+            h, count = args
+            if h < A:
+                take(hops[h - 1], count)
+        elif kind == "grad":
+            if grads:
+                gradient()
+        elif kind in queues:
+            take(queues[kind], args[0] if args else len(queues[kind]))
+        else:
+            if kind == "right4":
+                take(send, K)
+                while grads:
+                    gradient()
+            steps.append((kind,))
+    return steps
 
 
 def kernel(
@@ -94,7 +120,7 @@
     out_ref, ne_ref,
     xv, xg, xt, gg, wq, bas, bz, ball, ev, eh, el, ysend, yrecv, up_s, up_r, dn_s, dn_r,
     ls, lz, left_s, left_r, zs, zr, rp, rq, rs, rw, rz, rown, rall, own,
-    in_sem, send_sem, recv_sem, gs_sem, gr_sem, yr_sem, rs_sem, rr_sem,
+    in_sem, send_sem, recv_sem, gs_sem, gr_sem, rs_sem, rr_sem,
 ):
     o = lax.axis_index("outer")
     c = lax.axis_index("chip")
@@ -291,7 +317,7 @@
     def y_copy(d, k):
         return remote(
             ysend.at[d - 1, :, cols[k]], yrecv.at[d - 1, :, cols[k]],
-            family("y")[0], yr_sem.at[d - 1, k], member(0, d),
+            *family("y"), member(0, d),
         )
 
     def gradient_chunk(k):
@@ -301,10 +327,12 @@
             y_copy(d, k).start()
         ne_ref[:, cols[k]] = dot(xt[shard_of(b), :], gg[:, cols[k]], 1, 0)
 
+    def y_in():
+        y_all.wait_recv()
+
     def merge_chunk(k):
         part = ne_ref[:, cols[k]]
         for d in range(1, B):
-            y_copy(d, k).wait_recv()
             part = part + yrecv[d - 1, :, cols[k]].astype(F32)
         ne_ref[:, cols[k]] = part / TOK_DEV + ev[:, cols[k]]
 
@@ -336,11 +364,17 @@
             return jnp.logical_and(a >= 1, a - 1 + r < A)
         return jnp.logical_and(a + 1 < A, a + 1 - r >= 0)
 
-    def out_piece(direction, r, k, first):
+    def o_outer(direction):
+        return a == A - 2 if direction == 0 else a == 1
+
+    def out_piece(direction, r, k, first, outer=None):
         s_buf, r_buf = (up_s, up_r) if direction == 0 else (dn_s, dn_r)
         leads = o_first(direction)
         if not first:
             leads = jnp.logical_not(leads)
+        if outer is not None:
+            bound = o_outer(direction)
+            leads = jnp.logical_and(leads, bound if outer else jnp.logical_not(bound))
 
         @pl.when(jnp.logical_and(o_sends(direction, r), leads))
         def _():
@@ -396,6 +430,14 @@
             out_piece(direction, r, k, False)
 
     j_copies = along(lambda t: ls.at[t], lz.at[a], "j")
+    def inner_piece(k):
+        for direction in range(2):
+            out_piece(direction, 1, k, False, False)
+
+    def outer_piece(k):
+        for direction in range(2):
+            out_piece(direction, 1, k, False, True)
+
     l_copies = across(lambda do, db: left_s, lambda j, db: left_r.at[j], "l")
     z_copies = along(lambda t: zs.at[t], zr.at[a], "z")
     h_copies = across(
@@ -485,30 +527,26 @@
         for k in range(K):
             own[:, cols[k]] = dot(xg[rows_of(a), :], wq[:, cols[k]], 1, 0)
 
-    def wave(step):
-        for h in range(1, A):
-            k = step - h
-            if 0 <= k < K:
-                for direction in range(2):
-                    @pl.when(g_gets(direction, h))
-                    def _():
-                        g_arrival(direction, h, k).wait_recv()
-                    if h + 1 < A:
-                        @pl.when(g_sends(direction, h + 1))
-                        def _():
-                            g_copy(direction, h + 1, k).start()
-        k = step - 1 + AHEAD
-        if k < K:
-            g_first(k)
-        k = step - (A - 1)
-        if 0 <= k < K:
-            gradient_chunk(k)
+    def hop(h, k):
+        for direction in range(2):
+            @pl.when(g_gets(direction, h))
+            def _():
+                g_arrival(direction, h, k).wait_recv()
+            if h + 1 < A:
+                @pl.when(g_sends(direction, h + 1))
+                def _():
+                    g_copy(direction, h + 1, k).start()
+
+    def grad(k):
+        gradient_chunk(k)
 
     actions = {
-        "basis": basis_pass, "left0": left_part, "x": x_in, "wave": wave, "weights": weights_in, "mates": mates_in, "left1": left_line,
+        "basis": basis_pass, "left0": left_part, "x": x_in, "send": g_first, "hop": hop,
+        "grad": grad, "weights": weights_in, "mates": mates_in, "left1": left_line,
         "left2": left_done, "right1": right_part, "right2": right_group,
         "right3": right_line, "right4": right_all, "own": own_out,
-        "first": first_piece, "rest": rest_piece, "merge": merge_chunk,
+        "first": first_piece, "rest": rest_piece,
+        "inner": inner_piece, "outer": outer_piece, "y": y_in, "merge": merge_chunk,
     }
     for kind, *args in plan_of(A, K):
         actions[kind](*args)
@@ -564,6 +602,17 @@
                     place, place, rs_sem.at[direction, h - 1], rr_sem.at[0, 0],
                     {"chip": c + step * B},
                 ).wait_send()
+
+
+def store(out_vmem, ne_vmem, out_hbm, ne_hbm, sem):
+    copies = [
+        pltpu.make_async_copy(ne_vmem, ne_hbm, sem.at[0]),
+        pltpu.make_async_copy(out_vmem, out_hbm, sem.at[1]),
+    ]
+    for cp in copies:
+        cp.start()
+    for cp in copies:
+        cp.wait()
 
 
 def shards(inputs, out_grads, weight, start_basis, error_buffer):
@@ -621,7 +670,7 @@
             pltpu.VMEM((B, A, R, N), BF16),
             pltpu.VMEM((T, N), F32),
             dma((7,)), dma((len(FAMILIES),)), dma((len(FAMILIES) + PIECES - 1,)),
-            dma((2, A - 1)), dma((A, K)), dma((B - 1, K)), dma((2, A - 1)), dma((A + 1, K)),
+            dma((2, A - 1)), dma((A, K)), dma((2, A - 1)), dma((A + 1, K)),
         ],
         compiler_params=pltpu.CompilerParams(
             collective_id=0, has_side_effects=True, vmem_limit_bytes=40 * 1024 * 1024
@@ -631,6 +680,19 @@
         pltpu.with_memory_space_constraint(t, pltpu.HBM)
         for t in (inputs, out_grads, weight, start_basis, error_buffer[0])
     ])
+    hbm_out = pl.BlockSpec(memory_space=pltpu.HBM)
+    outputs, new_error = pl.pallas_call(
+        store,
+        out_shape=(
+            jax.ShapeDtypeStruct((T, N), BF16),
+            jax.ShapeDtypeStruct((S, N), F32),
+        ),
+        in_specs=[vmem] * 2,
+        out_specs=(hbm_out, hbm_out),
+        scratch_shapes=[dma((2,))],
+        compiler_params=pltpu.CompilerParams(vmem_limit_bytes=8 * 1024 * 1024),
+        name="store",
+    )(outputs, new_error)
     return outputs, new_error[None]
 
 

time: 74.3 us -> 71 us (0.956)
  local copies, waits for them, and re-layouts: 2.11 us -> 0 us
  Pallas kernels: 71.4 us -> 69.9 us
    pallas_call x1, Pallas kernels: 71.4 us -> 68.4 us  [shards(): pl.pallas_call(functools.partial(kernel, A, B, PODS), out_shape=(pltpu.VM...]
    unnamed x2 -> x0, local copies, waits for them, and re-layouts: 2.11 us -> none
    pallas_call x0 -> x1, Pallas kernels: none -> 1.5 us  [shards(): pl.pallas_call(store, out_shape=(jax.ShapeDtypeStruct((T, N), BF16), jax....]
where the time goes in v4:
time: 71 us; the launch traced here: 70.7 us
  Pallas kernels  69.9 us (98%)
  between operations  0.8 us (1%)
    pallas_call x1, Pallas kernels, shards(): pl.pallas_call(functools.partial(kernel, A, B, PODS), out_shape=(pltpu.VM...  68.4 us
    pallas_call x1, Pallas kernels, shards(): pl.pallas_call(store, out_shape=(jax.ShapeDtypeStruct((T, N), BF16), jax....  1.5 us

profile of v4, /device:TPU:0, one launch (start us, length us, event | category | flops | bytes accessed | tf_op | source)
XLA Modules:
  0.0 70.7 jit_solution(3585508415532560877)
XLA Ops:
  0.6 68.4 %step.1 = (bf16[128,2048]{1,0:T(8,128)(2,1)S(1)}, f32[256,2048]{1,0:T(8,128)S(1)}) custom-call(bf16[128,2048]{1,0:T(8,128)(2,1)} %x_hbm.1, bf16[128,2048]{1,0:T(8,128)(2,1)} %g_hbm.1, bf16[256,2048]{1,0:T(8,128)(2,1)} %w_hbm.1, f32[8,2048]{1,0:T(8,128)} %basis_hbm.1, f32[256,2048]{1,0:T(8,128)} %bitcast.2), custom_call_target="tpu_custom_call" | custom-call | tf_op jit(solution)/shard_map/step/pallas_call | solution.py:632
  69.0 1.5 %store.1 = (bf16[128,2048]{1,0:T(8,128)(2,1)}, f32[256,2048]{1,0:T(8,128)}) custom-call(bf16[128,2048]{1,0:T(8,128)(2,1)S(1)} %get-tuple-element.6.out_vmem, f32[256,2048]{1,0:T(8,128)S(1)} %get-tuple-element.7.ne_vmem), custom_call_target="tpu_custom_call" | custom-call | tf_op jit(solution)/shard_map/store/pallas_call | solution.py:684

commit v5 on v4

--- a/solution.py
+++ b/solution.py
@@ -61,20 +61,25 @@
 
 
 PLAN = (
-    ("basis",), ("send", 1), ("hop", 1, 1), ("left0",), ("x",), ("hop", 1, 1), ("send", 1),
-    ("hop", 1, 1), ("send", 1), ("hop", 2, 1), ("weights",), ("hop", 1, 1), ("send",),
-    ("hop", 2, 1), ("mates",), ("first", 3), ("grad",), ("hop", 1, 1), ("left1",), ("first", 3),
-    ("hop", 2, 1), ("grad",), ("hop", 1, 1), ("left2",), ("own",), ("hop", 2, 1), ("hop", 1, 1),
-    ("first", 4), ("grad",), ("hop", 1, 1), ("hop", 2, 1), ("rest", 2), ("right1",), ("first", 2),
-    ("grad",), ("hop", 2, 1), ("rest", 3), ("first", 1), ("grad",), ("right2",), ("hop", 2, 1),
-    ("rest", 3), ("first", 4), ("grad",), ("hop", 2, 1), ("outer", 2), ("first", 1), ("right3",),
-    ("grad",), ("rest", 3), ("first", 3), ("outer", 3), ("grad",), ("rest", 2), ("right4",),
-    ("first",), ("outer",), ("rest",), ("y",), ("merge",),
+    ("hop", 1, 1), ("out", 1), ("basis",), ("out", 2), ("into", 1), ("x",), ("hop", 2, 1),
+    ("hop", 1, 1), ("left0",), ("weights",), ("mates",), ("hop", 1, 1), ("into", 1),
+    ("hop", 1, 1), ("first", 2), ("hop", 2, 1), ("hop", 1, 1), ("into", 1), ("first", 1),
+    ("left1",), ("first", 1), ("rest", 1), ("first", 2), ("hop", 2, 1), ("grad",), ("left2",),
+    ("rest", 1), ("hop", 1, 1), ("grad",), ("hop", 2, 1), ("into", 1), ("first", 2),
+    ("hop", 2, 1), ("hop", 1, 1), ("rest", 2), ("first", 1), ("outer", 1), ("grad",),
+    ("first", 1), ("right1",), ("rest", 1), ("first", 2), ("rest", 1), ("outer", 1), ("out", 1),
+    ("grad",), ("hop", 2, 1), ("grad",), ("hop", 2, 1), ("right2",), ("first", 1), ("hop", 1, 1),
+    ("first", 2), ("rest", 1), ("first", 1), ("rest", 1), ("own",), ("grad",), ("grad",),
+    ("right3",), ("first", 2), ("hop", 2, 1), ("outer", 1), ("rest", 1), ("outer", 1),
+    ("rest", 2), ("outer", 1), ("first", 3), ("outer", 1), ("first", 1), ("outer", 1),
+    ("rest", 1), ("grad",), ("outer", 1), ("rest", 2), ("first", 1), ("rest", 2), ("first", 1),
+    ("right4",), ("y",), ("merge",),
 )
 
 
 def plan_of(A, K):
-    send = [("send", k) for k in range(AHEAD, K)]
+    out = [("out", k) for k in range(AHEAD, K)]
+    into = [("into", k) for k in range(AHEAD, K)]
     hops = [[("hop", h, k) for k in range(K)] for h in range(1, A)]
     grads = list(range(K))
     firsts = [("first", r, k) for r in range(A - 1, 0, -1) for k in range(K)]
@@ -82,7 +87,7 @@
     rests += [("inner", k) for k in range(K)]
     outers = [("outer", k) for k in range(K)]
     merges = [("merge", k) for k in range(K)]
-    queues = {"send": send, "first": firsts, "rest": rests, "outer": outers, "merge": merges}
+    queues = {"out": out, "into": into, "first": firsts, "rest": rests, "outer": outers, "merge": merges}
     steps = []
 
     def take(queue, count):
@@ -106,8 +111,9 @@
         elif kind in queues:
             take(queues[kind], args[0] if args else len(queues[kind]))
         else:
-            if kind == "right4":
-                take(send, K)
+            if kind == "y":
+                take(out, K)
+                take(into, K)
                 while grads:
                     gradient()
             steps.append((kind,))
@@ -285,9 +291,26 @@
     w_all = whole(wq.at[rest, pl.ds(0, PIECES * WN)], "w")
     m_all = whole(wq.at[rest, pl.ds(0, PIECES * WN)], "m")
 
+    def inward(direction):
+        if direction == 0:
+            return jnp.logical_and(a >= 1, a + 1 < A - 1)
+        return jnp.logical_and(a <= A - 2, a - 1 >= 1)
+
     def g_first(k):
         for direction in range(2):
             @pl.when(g_sends(direction, 1))
+            def _():
+                g_copy(direction, 1, k).start()
+
+    def g_out(k):
+        for direction in range(2):
+            @pl.when(jnp.logical_and(g_sends(direction, 1), jnp.logical_not(inward(direction))))
+            def _():
+                g_copy(direction, 1, k).start()
+
+    def g_into(k):
+        for direction in range(2):
+            @pl.when(jnp.logical_and(g_sends(direction, 1), inward(direction)))
             def _():
                 g_copy(direction, 1, k).start()
 
@@ -541,7 +564,7 @@
         gradient_chunk(k)
 
     actions = {
-        "basis": basis_pass, "left0": left_part, "x": x_in, "send": g_first, "hop": hop,
+        "basis": basis_pass, "left0": left_part, "x": x_in, "out": g_out, "into": g_into, "hop": hop,
         "grad": grad, "weights": weights_in, "mates": mates_in, "left1": left_line,
         "left2": left_done, "right1": right_part, "right2": right_group,
         "right3": right_line, "right4": right_all, "own": own_out,
@@ -563,6 +586,8 @@
             [rall[d, t, :, cols[k]].astype(F32) for d in range(B) for t in range(A)], axis=0
         )
         delta = dot(z_wide[0], stack(rights, rights), 0, 0)
+        own[:, cols[k]] = own[:, cols[k]] - LEARNING_RATE * delta
+    for k in range(K):
         for direction in range(2):
             r_buf = up_r if direction == 0 else dn_r
 
@@ -573,8 +598,8 @@
             @pl.when(jnp.logical_not(o_gets(direction, 1)))
             def _():
                 r_buf[0, :, cols[k]] = jnp.zeros((T, CN), BF16)
-        mine = own[:, cols[k]] + up_r[0, :, cols[k]].astype(F32) + dn_r[0, :, cols[k]].astype(F32)
-        out_ref[:, cols[k]] = (mine - LEARNING_RATE * delta).astype(BF16)
+        both = up_r[0, :, cols[k]].astype(F32) + dn_r[0, :, cols[k]].astype(F32)
+        out_ref[:, cols[k]] = (own[:, cols[k]] + both).astype(BF16)
 
     for cp in (
         x_all, c_all, v_all, b_all, w_all, j_all, l_all, z_all, h_all, t_all, p_all, a_all, f_all,

time: 71 us -> 70.1 us (0.987)
  Pallas kernels: 69.9 us -> 68.9 us
    pallas_call x1, Pallas kernels: 68.4 us -> 67.4 us  [shards(): pl.pallas_call(functools.partial(kernel, A, B, PODS), out_shape=(pltpu.VM...]
where the time goes in v5:
time: 70.1 us; the launch traced here: 69.7 us
  Pallas kernels  68.9 us (98%)
  between operations  0.8 us (1%)
    pallas_call x1, Pallas kernels, shards(): pl.pallas_call(functools.partial(kernel, A, B, PODS), out_shape=(pltpu.VM...  67.4 us
    pallas_call x1, Pallas kernels, shards(): pl.pallas_call(store, out_shape=(jax.ShapeDtypeStruct((T, N), BF16), jax....  1.5 us

profile of v5, /device:TPU:0, one launch (start us, length us, event | category | flops | bytes accessed | tf_op | source)
XLA Modules:
  0.0 69.7 jit_solution(15705073152603751793)
XLA Ops:
  0.6 67.4 %step.1 = (bf16[128,2048]{1,0:T(8,128)(2,1)S(1)}, f32[256,2048]{1,0:T(8,128)S(1)}) custom-call(bf16[128,2048]{1,0:T(8,128)(2,1)} %x_hbm.1, bf16[128,2048]{1,0:T(8,128)(2,1)} %g_hbm.1, bf16[256,2048]{1,0:T(8,128)(2,1)} %w_hbm.1, f32[8,2048]{1,0:T(8,128)} %basis_hbm.1, f32[256,2048]{1,0:T(8,128)} %bitcast.2), custom_call_target="tpu_custom_call" | custom-call | tf_op jit(solution)/shard_map/step/pallas_call | solution.py:657
  68.0 1.5 %store.1 = (bf16[128,2048]{1,0:T(8,128)(2,1)}, f32[256,2048]{1,0:T(8,128)}) custom-call(bf16[128,2048]{1,0:T(8,128)(2,1)S(1)} %get-tuple-element.6.out_vmem, f32[256,2048]{1,0:T(8,128)S(1)} %get-tuple-element.7.ne_vmem), custom_call_target="tpu_custom_call" | custom-call | tf_op jit(solution)/shard_map/store/pallas_call | solution.py:709

commit v6 on v5

--- a/solution.py
+++ b/solution.py
@@ -12,7 +12,7 @@
 CHUNKS = 8
 AHEAD = 4
 PIECES = 2
-FAMILIES = "abcfhjlmptvxyzw"
+FAMILIES = "abcfhjklmptuvxyzw"
 F32 = jnp.float32
 BF16 = jnp.bfloat16
 
@@ -61,25 +61,27 @@
 
 
 PLAN = (
-    ("hop", 1, 1), ("out", 1), ("basis",), ("out", 2), ("into", 1), ("x",), ("hop", 2, 1),
-    ("hop", 1, 1), ("left0",), ("weights",), ("mates",), ("hop", 1, 1), ("into", 1),
-    ("hop", 1, 1), ("first", 2), ("hop", 2, 1), ("hop", 1, 1), ("into", 1), ("first", 1),
-    ("left1",), ("first", 1), ("rest", 1), ("first", 2), ("hop", 2, 1), ("grad",), ("left2",),
-    ("rest", 1), ("hop", 1, 1), ("grad",), ("hop", 2, 1), ("into", 1), ("first", 2),
-    ("hop", 2, 1), ("hop", 1, 1), ("rest", 2), ("first", 1), ("outer", 1), ("grad",),
-    ("first", 1), ("right1",), ("rest", 1), ("first", 2), ("rest", 1), ("outer", 1), ("out", 1),
-    ("grad",), ("hop", 2, 1), ("grad",), ("hop", 2, 1), ("right2",), ("first", 1), ("hop", 1, 1),
-    ("first", 2), ("rest", 1), ("first", 1), ("rest", 1), ("own",), ("grad",), ("grad",),
-    ("right3",), ("first", 2), ("hop", 2, 1), ("outer", 1), ("rest", 1), ("outer", 1),
-    ("rest", 2), ("outer", 1), ("first", 3), ("outer", 1), ("first", 1), ("outer", 1),
-    ("rest", 1), ("grad",), ("outer", 1), ("rest", 2), ("first", 1), ("rest", 2), ("first", 1),
-    ("right4",), ("y",), ("merge",),
+    ("basis",), ("hop", 1, 1), ("left0",), ("out", 1), ("hop", 1, 1), ("edge", 1), ("lefthop", 1),
+    ("weights",), ("edge", 1), ("hop", 1, 1), ("into", 1), ("hop", 1, 1), ("into", 1), ("x",),
+    ("mates",), ("hop", 2, 1), ("into", 1), ("lefthop", 2), ("out", 1), ("first", 1),
+    ("hop", 2, 1), ("hop", 1, 1), ("first", 1), ("hop", 2, 1), ("first", 2), ("left1",),
+    ("first", 2), ("out", 1), ("grad",), ("grad",), ("first", 1), ("rest", 1), ("hop", 2, 1),
+    ("left2",), ("rest", 1), ("edge", 1), ("hop", 1, 1), ("out", 1), ("first", 1), ("grad",),
+    ("into", 1), ("rest", 1), ("edge", 1), ("hop", 2, 1), ("first", 1), ("right1",), ("first", 2),
+    ("hop", 1, 1), ("hop", 2, 1), ("outer", 1), ("rest", 1), ("first", 1), ("hop", 1, 1),
+    ("outer", 1), ("rest", 1), ("grad",), ("right2",), ("rest", 1), ("first", 2), ("hop", 2, 1),
+    ("first", 1), ("grad",), ("righthop", 1), ("rest", 2), ("first", 1), ("hop", 2, 1), ("grad",),
+    ("first", 1), ("rest", 1), ("righthop", 2), ("outer", 1), ("grad",), ("own",), ("right3",),
+    ("first", 1), ("outer", 1), ("first", 1), ("rest", 1), ("first", 1), ("outer", 1),
+    ("rest", 3), ("grad",), ("first", 3), ("outer", 2), ("first", 1), ("right4",), ("rest", 1),
+    ("outer", 1), ("rest", 2), ("y",), ("merge",),
 )
 
 
 def plan_of(A, K):
     out = [("out", k) for k in range(AHEAD, K)]
     into = [("into", k) for k in range(AHEAD, K)]
+    edge = [("edge", k) for k in range(AHEAD, K)]
     hops = [[("hop", h, k) for k in range(K)] for h in range(1, A)]
     grads = list(range(K))
     firsts = [("first", r, k) for r in range(A - 1, 0, -1) for k in range(K)]
@@ -87,7 +89,7 @@
     rests += [("inner", k) for k in range(K)]
     outers = [("outer", k) for k in range(K)]
     merges = [("merge", k) for k in range(K)]
-    queues = {"out": out, "into": into, "first": firsts, "rest": rests, "outer": outers, "merge": merges}
+    queues = {"out": out, "into": into, "edge": edge, "first": firsts, "rest": rests, "outer": outers, "merge": merges}
     steps = []
 
     def take(queue, count):
@@ -108,12 +110,16 @@
         elif kind == "grad":
             if grads:
                 gradient()
+        elif kind[-3:] == "hop":
+            lines = range(1, A - 1) if args[0] == 0 else [args[0]]
+            steps.extend((kind, i) for i in lines if i < A - 1)
         elif kind in queues:
             take(queues[kind], args[0] if args else len(queues[kind]))
         else:
             if kind == "y":
                 take(out, K)
                 take(into, K)
+                take(edge, K)
                 while grads:
                     gradient()
             steps.append((kind,))
@@ -125,7 +131,7 @@
     x_hbm, g_hbm, w_hbm, basis_hbm, err_hbm,
     out_ref, ne_ref,
     xv, xg, xt, gg, wq, bas, bz, ball, ev, eh, el, ysend, yrecv, up_s, up_r, dn_s, dn_r,
-    ls, lz, left_s, left_r, zs, zr, rp, rq, rs, rw, rz, rown, rall, own,
+    ls, l_sum, l_up, l_dn, left_s, left_r, zs, zr, rp, rq, rs, r_sum, r_up, r_dn, rz, rown, rall, own,
     in_sem, send_sem, recv_sem, gs_sem, gr_sem, rs_sem, rr_sem,
 ):
     o = lax.axis_index("outer")
@@ -216,11 +222,9 @@
     c_all = whole(bz.at[lines], "c")
     v_all = whole(ball.at[pl.ds(0, B - 1), :, :, pl.ds(0, NP)], "v")
     b_all = whole(ball.at[:, :, :, others], "b")
-    j_all = whole(ls.at[lines], "j")
     l_all = whole(left_r, "l")
     z_all = whole(zs.at[lines], "z")
     h_all = whole(rq, "h")
-    t_all = whole(rs.at[lines], "t")
     p_all = whole(rown.at[:, others], "p")
     a_all = whole(rz.at[lines], "a")
     f_all = whole(rq, "f")
@@ -304,7 +308,15 @@
 
     def g_out(k):
         for direction in range(2):
-            @pl.when(jnp.logical_and(g_sends(direction, 1), jnp.logical_not(inward(direction))))
+            last = a == A - 2 if direction == 0 else a == 1
+
+            @pl.when(jnp.logical_and(last, jnp.logical_and(a >= 1, a <= A - 2)))
+            def _():
+                g_copy(direction, 1, k).start()
+
+    def g_edge(k):
+        for direction in range(2):
+            @pl.when(a == 0 if direction == 0 else a == A - 1)
             def _():
                 g_copy(direction, 1, k).start()
 
@@ -408,6 +420,42 @@
                 part = part + r_buf[r, :, cols[k]].astype(F32)
             s_buf[r - 1, :, cols[k]] = part.astype(BF16)
             o_copy(direction, r, k).start()
+
+    def line_copy(hop, direction, src, dst, name):
+        part = pl.ds(hop + 1, A - 1 - hop) if direction == 0 else pl.ds(0, A - 1 - hop)
+        to = c + B if direction == 0 else c - B
+        return remote(src.at[part], dst.at[part], *family(name), {"chip": to})
+
+    def at_hop(hop, direction):
+        return a == hop if direction == 0 else a == A - 1 - hop
+
+    def line_hop(hop, own_part, sums, came, names):
+        for direction in range(2):
+            @pl.when(at_hop(hop, direction))
+            def _():
+                dst = came[direction]
+                if hop == 0:
+                    src = own_part
+                else:
+                    line_copy(hop - 1, direction, dst, dst, names[direction]).wait_recv()
+                    src = sums.at[direction]
+                    for t in range(hop + 1, A) if direction == 0 else range(A - 1 - hop):
+                        total = own_part[t].astype(F32) + dst[t].astype(F32)
+                        src[t] = total.astype(src.dtype)
+                line_copy(hop, direction, src, dst, names[direction]).start()
+
+    def line_end(came, names):
+        for direction in range(2):
+            @pl.when(at_hop(A - 1, direction))
+            def _():
+                dst = came[direction]
+                line_copy(A - 2, direction, dst, dst, names[direction]).wait_recv()
+
+    def left_hop(hop):
+        line_hop(hop, ls, l_sum, (l_up, l_dn), "jk")
+
+    def right_hop(hop):
+        line_hop(hop, rs, r_sum, (r_up, r_dn), "tu")
 
     def basis_pass():
         v_all.wait_recv()
@@ -427,8 +475,7 @@
                 row = (d * A + t) * R
                 shard = shard_of(t * B + (b + d) % B)
                 ls[t, d] = fold(dot(split(thin[row : row + R, :]), xv[:, shard], 1, 0)) / TOK_DEV
-        start(j_copies)
-        lz[a] = ls[a]
+        line_hop(0, ls, l_sum, (l_up, l_dn), "jk")
 
 
     def x_in():
@@ -452,7 +499,6 @@
         for direction in range(2):
             out_piece(direction, r, k, False)
 
-    j_copies = along(lambda t: ls.at[t], lz.at[a], "j")
     def inner_piece(k):
         for direction in range(2):
             out_piece(direction, 1, k, False, False)
@@ -467,7 +513,6 @@
         lambda do, db: rp.at[db, :, :, share_of((o + do) % PODS)],
         lambda j, db: rq.at[j], "h",
     )
-    t_copies = along(lambda t: rs.at[t], rw.at[a], "t")
     a_copies = along(lambda t: rz.at[a], rz.at[a], "a")
     p_copies = [
         remote(rz.at[a], rown.at[:, share_of(o)], *family("p"), member(do, 0))
@@ -478,11 +523,10 @@
     )
 
     def left_line():
-        j_all.wait_recv()
+        line_end((l_up, l_dn), "jk")
         for d in range(B):
-            part = lz[0, d]
-            for t in range(1, A):
-                part = part + lz[t, d]
+            part = ls[a, d] + jnp.where(a > 0, l_up[a, d], 0.0)
+            part = part + jnp.where(a < A - 1, l_dn[a, d], 0.0)
             left_s[d] = part + fed if d == 0 else part
         start(l_copies)
 
@@ -529,14 +573,12 @@
         for j in range(len(group)):
             right = right + rq[j].astype(F32)
         rs[...] = right.astype(BF16)
-        start(t_copies)
-        rw[a] = rs[a]
+        line_hop(0, rs, r_sum, (r_up, r_dn), "tu")
 
     def right_line():
-        t_all.wait_recv()
-        right = rw[0].astype(F32)
-        for t in range(1, A):
-            right = right + rw[t].astype(F32)
+        line_end((r_up, r_dn), "tu")
+        right = rs[a].astype(F32) + jnp.where(a > 0, r_up[a].astype(F32), 0.0)
+        right = right + jnp.where(a < A - 1, r_dn[a].astype(F32), 0.0)
         rz[a] = (right / PODS).astype(BF16)
         start(a_copies + p_copies)
         rown[:, share_of(o)] = rz[a]
@@ -564,12 +606,14 @@
         gradient_chunk(k)
 
     actions = {
-        "basis": basis_pass, "left0": left_part, "x": x_in, "out": g_out, "into": g_into, "hop": hop,
+        "basis": basis_pass, "left0": left_part, "x": x_in, "out": g_out, "into": g_into,
+        "edge": g_edge, "hop": hop,
         "grad": grad, "weights": weights_in, "mates": mates_in, "left1": left_line,
         "left2": left_done, "right1": right_part, "right2": right_group,
         "right3": right_line, "right4": right_all, "own": own_out,
         "first": first_piece, "rest": rest_piece,
-        "inner": inner_piece, "outer": outer_piece, "y": y_in, "merge": merge_chunk,
+        "inner": inner_piece, "outer": outer_piece, "y": y_in, "lefthop": left_hop, "righthop": right_hop,
+        "merge": merge_chunk,
     }
     for kind, *args in plan_of(A, K):
         actions[kind](*args)
@@ -602,12 +646,19 @@
         out_ref[:, cols[k]] = (own[:, cols[k]] + both).astype(BF16)
 
     for cp in (
-        x_all, c_all, v_all, b_all, w_all, j_all, l_all, z_all, h_all, t_all, p_all, a_all, f_all,
-        y_all,
+        x_all, c_all, v_all, b_all, w_all, l_all, z_all, h_all, p_all, a_all, f_all, y_all,
     ):
         cp.wait_send()
     if shared:
         m_all.wait_send()
+    for hop_index in range(A - 1):
+        for direction in range(2):
+            @pl.when(at_hop(hop_index, direction))
+            def _():
+                for own_part, names in ((ls, "jk"), (rs, "tu")):
+                    line_copy(
+                        hop_index, direction, own_part, own_part, names[direction]
+                    ).wait_send()
     for direction in range(2):
         for h in range(1, A):
             step = 1 if direction == 0 else -1
@@ -681,6 +732,8 @@
             pltpu.VMEM((A - 1, T, N), BF16),
             pltpu.VMEM((A - 1, T, N), BF16),
             pltpu.VMEM((A, B, R, S), F32),
+            pltpu.VMEM((2, A, B, R, S), F32),
+            pltpu.VMEM((A, B, R, S), F32),
             pltpu.VMEM((A, B, R, S), F32),
             pltpu.VMEM((B, R, S), F32),
             pltpu.VMEM((G - 1, B, R, S), F32),
@@ -688,6 +741,8 @@
             pltpu.VMEM((A, B * R, T), F32),
             pltpu.VMEM((B, A, R, N), BF16),
             pltpu.VMEM((G - 1, A, R, N // PODS), BF16),
+            pltpu.VMEM((A, R, N // PODS), BF16),
+            pltpu.VMEM((2, A, R, N // PODS), BF16),
             pltpu.VMEM((A, R, N // PODS), BF16),
             pltpu.VMEM((A, R, N // PODS), BF16),
             pltpu.VMEM((A, R, N // PODS), BF16),

time: 70.1 us -> 69.6 us (level)
  no operation moved by 1% of the time
where the time goes in v6:
time: 69.6 us; the launch traced here: 69.4 us
  Pallas kernels  68.6 us (99%)
  between operations  0.8 us (1%)
    pallas_call x1, Pallas kernels, shards(): pl.pallas_call(functools.partial(kernel, A, B, PODS), out_shape=(pltpu.VM...  67.1 us
    pallas_call x1, Pallas kernels, shards(): pl.pallas_call(store, out_shape=(jax.ShapeDtypeStruct((T, N), BF16), jax....  1.5 us

profile of v6, /device:TPU:0, one launch (start us, length us, event | category | flops | bytes accessed | tf_op | source)
XLA Modules:
  0.0 69.4 jit_solution(4947126404780036912)
XLA Ops:
  0.6 67.1 %step.1 = (bf16[128,2048]{1,0:T(8,128)(2,1)S(1)}, f32[256,2048]{1,0:T(8,128)S(1)}) custom-call(bf16[128,2048]{1,0:T(8,128)(2,1)} %x_hbm.1, bf16[128,2048]{1,0:T(8,128)(2,1)} %g_hbm.1, bf16[256,2048]{1,0:T(8,128)(2,1)} %w_hbm.1, f32[8,2048]{1,0:T(8,128)} %basis_hbm.1, f32[256,2048]{1,0:T(8,128)} %bitcast.2), custom_call_target="tpu_custom_call" | custom-call | tf_op jit(solution)/shard_map/step/pallas_call | solution.py:708
  67.7 1.5 %store.1 = (bf16[128,2048]{1,0:T(8,128)(2,1)}, f32[256,2048]{1,0:T(8,128)}) custom-call(bf16[128,2048]{1,0:T(8,128)(2,1)S(1)} %get-tuple-element.6.out_vmem, f32[256,2048]{1,0:T(8,128)S(1)} %get-tuple-element.7.ne_vmem), custom_call_target="tpu_custom_call" | custom-call | tf_op jit(solution)/shard_map/store/pallas_call | solution.py:764
